TPU v7x, 256 devices: a whole 4x4x8 slice. The times are simulated.
256 devices in a mesh: section: 8 (over x, z_lo), dp: 32 (over y, z_hi, core).
Axes of the slice: x: 4, y: 4, z: 8 (z_hi: 4, z_lo: 2; z = z_hi * 2 + z_lo), core: 2. Of those that a mesh axis runs over, the one named last changes fastest.
Arguments:
- activations: bfloat16 [64, 512, 4608], P('section', 'dp'), may hold values from -6 to 6
- section_sources: int32 [64], replicated, may hold values from 0 to 63, as said below
- accumulators: float32 [1024, 16, 4608], P('dp', 'section'), may hold values from -6 to 6
- block_sources: int32 [1024], replicated, may hold values from 0 to 1023, as said below
- loss_terms: float32 [8, 32], P('section', 'dp'), may hold values from 0.35 to 6
- pre_gain: float32 [8, 4608], P('section'), may hold values from 0.1 to 1.9
- query_weight: bfloat16 [8, 4608, 4096], P('section', None, 'dp'), may hold values from -0.09375 to 0.09375
- keyval_weight: bfloat16 [8, 4608, 4096], P('section', None, 'dp'), may hold values from -0.09375 to 0.09375
- output_weight: bfloat16 [8, 4096, 4608], P('section', 'dp'), may hold values from -0.09375 to 0.09375
- post_gain: float32 [8, 4608], P('section'), may hold values from 0.1 to 1.9
Outputs:
- new_activations: bfloat16 [64, 512, 4608], P('section', 'dp')
- new_accumulators: float32 [1024, 16, 4608], P('dp', 'section')
- check_out: bfloat16 [8, 512, 4608], P('section', 'dp')
Inputs may be any that keep to these rules, and one draw needn't show every extreme that they name: `section_sources`: A permutation; each old section's micro-batches fill 1 slots of each new section. `block_sources`: A permutation; each old data index's blocks fill 1 block of each new data index.
All inputs are finite; a program needn't handle non-finite values.
Results may differ from a plain program's by a relative error of at most 0.014.
Values may be sent and summed in bfloat16 or wider, within the bound.
A program may use at most 64 MiB of HBM per device.

v0:
```python
import jax
import jax.numpy as jnp
from jax import lax
from jax.sharding import PartitionSpec as P

D = 4608


def sent_together(arrays, axis, split_dim, concat_dim, along):
    columns = [a.reshape(*a.shape[:along], -1) for a in arrays]
    both = jnp.concatenate(columns, axis=along)
    result, at, finished = (
        lax.all_to_all(both, axis, split_axis=split_dim, concat_axis=concat_dim, tiled=True),
        0,
        [],
    )
    for a, column in zip(arrays, columns):
        piece = result[..., at : at + column.shape[along]]
        finished.append(piece.reshape(*piece.shape[:along], *a.shape[along:]))
        at += column.shape[along]
    return tuple(finished)


def partner(value, axis, stride):
    mask = 2**stride
    pairs = [(source, source ^ mask) for source in range(lax.axis_size(axis))]
    return lax.ppermute(value, axis, pairs)


def rms_norm(values, gain):
    meansq = jnp.mean(values * values, axis=-1, keepdims=True)
    return values * lax.rsqrt(meansq + 1e-06) * gain


def rotary(values, positions):
    width = values.shape[-1]
    middle = width // 2
    counter = jnp.arange(middle, dtype=jnp.float32)
    freqs = 10000.0 ** (-2.0 * counter / width)
    angles = positions.astype(jnp.float32)[:, None] * freqs[None, :]
    cosine = jnp.cos(angles)
    sine = jnp.sin(angles)
    first = values[..., :middle]
    second = values[..., middle:]
    return jnp.concatenate(
        [first * cosine - second * sine, second * cosine + first * sine], axis=-1
    )


def plan_routes(sources, own_index, groups, per_group):
    per_peer = per_group // groups
    table = sources.reshape(groups, per_group)
    owners = table // per_group
    places = table % per_group
    slot_ids = jnp.arange(per_group, dtype=jnp.int32)
    sort_keys = jnp.where(owners == own_index, slot_ids[None, :], slot_ids[None, :] + per_group)
    ranking = jnp.argsort(sort_keys, axis=1)[:, :per_peer]
    send_index = jnp.take_along_axis(places, ranking, axis=1).reshape(-1)
    my_owners = lax.dynamic_slice_in_dim(owners, own_index, 1, 0)[0]
    earlier = (my_owners[None, :] == my_owners[:, None]) & (slot_ids[None, :] < slot_ids[:, None])
    earlier_count = jnp.sum(earlier.astype(jnp.int32), axis=1)
    recv_index = my_owners * per_peer + earlier_count
    return (send_index, recv_index)


def on_device(
    activations,
    section_sources,
    accumulators,
    block_sources,
    loss_terms,
    pre_gain,
    query_weight,
    keyval_weight,
    output_weight,
    post_gain,
):
    sections = lax.axis_size("section")
    section_index = lax.axis_index("section")
    mb_local = activations.shape[0]
    send_index, recv_index = plan_routes(section_sources, section_index, sections, mb_local)
    outgoing = jnp.take(activations, send_index, axis=0)
    incoming = lax.all_to_all(outgoing, "section", split_axis=0, concat_axis=0, tiled=True)
    moved = jnp.take(incoming, recv_index, axis=0)
    data_ranks = lax.axis_size("dp")
    data_index = lax.axis_index("dp")
    blk_local = accumulators.shape[0]
    per_peer = blk_local // data_ranks
    block_send, block_recv = plan_routes(block_sources, data_index, data_ranks, blk_local)
    outgoing_blocks = jnp.take(accumulators, block_send, axis=0)
    term_rows = jnp.broadcast_to(loss_terms, (blk_local, 1))
    incoming_blocks, incoming_terms = tuple(
        (
            part.astype(jnp.float32)
            for part in sent_together(
                (outgoing_blocks.astype(jnp.bfloat16), term_rows.astype(jnp.bfloat16)),
                "dp",
                0,
                0,
                1,
            )
        )
    )
    scale_sum = jnp.sum(incoming_terms[::per_peer, 0])
    factor = data_ranks / scale_sum
    new_accumulators = jnp.take(incoming_blocks, block_recv, axis=0) * factor
    checked = moved[0]
    head_size = query_weight.shape[2]
    is_even = data_index % 2 == 0
    w_query = query_weight[0]
    w_keyval = keyval_weight[0]
    gain_pre = pre_gain[0]
    block_rows = lax.all_gather(checked, "dp", axis=0, tiled=True)
    row_count = block_rows.shape[0]
    positions = jnp.arange(row_count, dtype=jnp.int32)
    normed = rms_norm(block_rows.astype(jnp.float32), gain_pre).astype(jnp.bfloat16)
    queries = jnp.dot(normed, w_query, preferred_element_type=jnp.float32)
    own_proj = jnp.dot(normed, w_keyval, preferred_element_type=jnp.float32)
    queries = rotary(queries, positions)
    own_proj = jnp.where(is_even, rotary(own_proj, positions), own_proj)
    projected = jnp.concatenate([queries, own_proj], axis=1).astype(jnp.bfloat16)
    queries = projected[:, :head_size]
    own_kv = projected[:, head_size:]
    partner_kv = partner(own_kv, "dp", 0)
    key_rows = jnp.where(is_even, own_kv, partner_kv)
    value_rows = jnp.where(is_even, partner_kv, own_kv)
    length = projected.shape[0]
    positions = jnp.arange(length, dtype=jnp.int32)
    scale_factor = (D / data_ranks) ** (-0.5)
    scores = (
        lax.dot_general(
            queries, key_rows, (((1,), (1,)), ((), ())), preferred_element_type=jnp.float32
        )
        * scale_factor
    )
    capped = 50.0 * jnp.tanh(scores / 50.0)
    causal = positions[None, :] <= positions[:, None]
    expd = jnp.where(causal, jnp.exp(capped), 0.0)
    denominator = jnp.sum(expd, axis=-1, keepdims=True)
    probs = expd.astype(jnp.bfloat16)
    numer = jnp.dot(probs, value_rows, preferred_element_type=jnp.float32)
    attended = (numer / denominator).astype(jnp.bfloat16)
    w_output = output_weight[0]
    summed = lax.psum_scatter(
        jnp.dot(attended, w_output, preferred_element_type=jnp.float32).astype(jnp.bfloat16),
        "dp",
        scatter_dimension=0,
        tiled=True,
    ).astype(jnp.float32)
    check_out = (checked.astype(jnp.float32) + rms_norm(summed, post_gain[0])).astype(jnp.bfloat16)
    return (moved, new_accumulators, check_out[None, :, :])


def solution(mesh):
    placed = (
        P("section", "dp", None),
        P(),
        P("dp", "section", None),
        P(),
        P("section", "dp"),
        P("section", None),
        P("section", None, "dp"),
        P("section", None, "dp"),
        P("section", "dp", None),
        P("section", None),
    )
    return jax.shard_map(
        on_device,
        mesh=mesh,
        in_specs=placed,
        out_specs=(P("section", "dp", None), P("dp", "section", None), P("section", "dp", None)),
        check_vma=False,
    )
```

profile of v0, /device:TPU:1, one launch (start us, length us, event | category | flops | bytes accessed | tf_op | source)
XLA Modules:
  0.0 223.3 jit_solution(8892449664727114092)
XLA Ops:
  7.2 0.8 reshape.111
  8.0 0.1 copy.20
  8.1 0.7 sort.34
  8.8 0.6 gather_fusion
  9.5 1.9 gather_fusion.2
  11.4 1.2 broadcast_select_fusion.1
  12.6 6.2 %all-to-all-start = ((bf16[8,16,4608]{2,1,0:T(8,128)(2,1)}), bf16[8,16,4608]{2,1,0:T(8,128)(2,1)S(1)}, u32[]{:S(2)}, u32[]{:S(2)}) async-start(bf16[8,16,4608]{2,1,0:T(8,128)(2,1)} %broadcast_select_fusion.1), calls=%async_computation | async-start | bytes 2359296 | tf_op jit(solution)/shard_map/all_to_all | solution.py:83
  18.8 0.0 all-gather.3.cloned.1.call-start
  18.8 0.2 convert_reduce_fusion.2
  19.0 16.0 %all-to-all-done = bf16[8,16,4608]{2,1,0:T(8,128)(2,1)S(1)} async-done(((bf16[8,16,4608]{2,1,0:T(8,128)(2,1)}), bf16[8,16,4608]{2,1,0:T(8,128)(2,1)S(1)}, u32[]{:S(2)}, u32[]{:S(2)}) %all-to-all-start) | async-done | bytes 1179680 | tf_op jit(solution)/shard_map/all_to_all | solution.py:83
  35.0 0.6 gather_fusion.3
  35.7 0.2 broadcast_select_fusion
  35.9 1.0 copy-done.3
  36.9 0.7 slice.56
  37.6 0.0 reduce-scatter.2.cloned.1.call-start
  37.7 0.1 reshape.114
  37.8 0.1 copy.21
  37.9 0.8 sort.35
  38.7 0.7 gather_fusion.1
  39.5 61.9 %all-gather.3.cloned.1.call-done = bf16[1,512,4608]{2,1,0:T(8,128)(2,1)} async-done(((bf16[1,16,4608]{2,1,0:T(8,128)(2,1)}), bf16[1,512,4608]{2,1,0:T(8,128)(2,1)}) %all-gather.3.cloned.1.call-update) | async-done | bytes 4718608 | tf_op jit(solution)/shard_map/all_gather | solution.py:113
  101.4 3.5 %fusion = f32[512]{0:T(512)S(1)} fusion(bf16[1,512,4608]{2,1,0:T(8,128)(2,1)} %all-gather.3.cloned.1.call-done), kind=kLoop, calls=%fused_computation.8 | loop fusion | flops 7077376 | bytes 4720640 | tf_op jit(solution)/shard_map/reduce_sum | solution.py:31
  104.9 0.3 copy-done.1
  105.2 1.8 fusion.7
  107.0 0.6 fusion.35
  107.6 0.5 collective-permute-start
  108.1 1.8 fusion.9
  110.0 0.6 fusion.32
  110.5 0.4 fusion.56
  111.0 3.9 %convolution_convert_fusion = bf16[512,4608]{1,0:T(8,128)(2,1)} fusion(bf16[1,128,4608]{2,1,0:T(8,128)(2,1)S(1)} %copy-done, bf16[512,512]{0,1:T(8,128)(2,1)S(1)} %get-tuple-element.28, f32[512]{0:T(512)S(1)} %get-tuple-element.27, bf16[512,128]{0,1:T(8,128)(2,1)S(1)} %collective-permute-done, bf16[512,128]{0,1:T(8,128)(2,1)S(1)} %fusion.21, pred[]{:T(512)S(6)} %eq.57), kind=kOutput, calls=%fused_computation.11 | convolution fusion | flops 673644544 | bytes 6686721 | tf_op jit(solution)/shard_map/dot_general | solution.py:145
  115.0 1.2 copy-done.4
  116.2 1.8 gather_fusion.4
  118.0 0.6 select_convert_fusion
  118.6 0.1 copy.24
  119.4 2.0 copy.22
  121.3 6.5 %all-to-all-start.1 = ((bf16[32,1,9217]{2,1,0:T(2,128)(2,1)}), bf16[32,1,9217]{2,1,0:T(2,128)(2,1)S(1)}, u32[]{:S(2)}, u32[]{:S(2)}) async-start(bf16[32,1,9217]{2,1,0:T(2,128)(2,1)} %copy.22), calls=%async_computation.1 | async-start | bytes 2392064 | tf_op jit(solution)/shard_map/all_to_all | solution.py:13
  127.9 0.7 reduce.2
  128.6 0.2 convert_reduce_fusion.1
  128.8 30.9 %all-to-all-done.1 = bf16[32,1,9217]{2,1,0:T(2,128)(2,1)S(1)} async-done(((bf16[32,1,9217]{2,1,0:T(2,128)(2,1)}), bf16[32,1,9217]{2,1,0:T(2,128)(2,1)S(1)}, u32[]{:S(2)}, u32[]{:S(2)}) %all-to-all-start.1) | async-done | bytes 589920 | tf_op jit(solution)/shard_map/all_to_all | solution.py:13
  159.7 0.1 copy.26
  159.8 0.8 copy-done.2
  160.6 0.1 slice_convert_fusion
  160.7 1.0 reshape.118
  161.7 1.8 gather_fusion.5
  163.5 1.3 convert_reduce_fusion
  165.4 1.6 select_multiply_fusion
  167.0 46.5 %reduce-scatter.2.cloned.1.call-done = bf16[16,4608]{1,0:T(8,128)(2,1)} async-done(((bf16[512,4608]{1,0:T(8,128)(2,1)}), bf16[16,4608]{1,0:T(8,128)(2,1)}) %reduce-scatter.2.cloned.1.call-update) | async-done | bytes 147472 | tf_op jit(solution)/shard_map/reduce_scatter | solution.py:144
  213.6 1.1 fusion.17
  214.7 1.8 fusion.30
  (52 shorter events, 0.4 us)
Async XLA Ops:
  7.2 103.8 %copy-start = (bf16[1,128,4608]{2,1,0:T(8,128)(2,1)S(1)}, bf16[1,128,4608]{2,1,0:T(8,128)(2,1)}, u32[]{:S(2)}) copy-start(bf16[1,128,4608]{2,1,0:T(8,128)(2,1)} %param.22) | copy-start | bytes 3538948
  12.6 22.5 %all-to-all-start = ((bf16[8,16,4608]{2,1,0:T(8,128)(2,1)}), bf16[8,16,4608]{2,1,0:T(8,128)(2,1)S(1)}, u32[]{:S(2)}, u32[]{:S(2)}) async-start(bf16[8,16,4608]{2,1,0:T(8,128)(2,1)} %broadcast_select_fusion.1), calls=%async_computation | async-start | bytes 2359296 | tf_op jit(solution)/shard_map/all_to_all | solution.py:83
  18.8 82.6 %all-gather.3.cloned.1.call-start = ((), (), s32[]{:S(2)}) async-start(), calls=%async_computation.4 | async-start | bytes 4866048 | tf_op jit(solution)/shard_map/all_gather | solution.py:113
  35.7 2.0 copy-start.8
  35.7 2.2 copy-start.6
  35.9 1.0 copy-start.3
  36.9 68.0 %copy-start.9 = (bf16[1,4608,128]{2,1,0:T(8,128)(2,1)S(1)}, bf16[1,4608,128]{2,1,0:T(8,128)(2,1)}, u32[]{:S(2)}) copy-start(bf16[1,4608,128]{2,1,0:T(8,128)(2,1)} %param.21) | copy-start | bytes 3538948
  37.6 176.0 %reduce-scatter.2.cloned.1.call-start = ((), (), s32[]{:S(2)}) async-start(), calls=%async_computation.3 | async-start | bytes 4866048 | tf_op jit(solution)/shard_map/reduce_scatter | solution.py:144
  101.4 3.8 %copy-start.1 = (bf16[1,512,4608]{2,1,0:T(8,128)(2,1)S(1)}, bf16[1,512,4608]{2,1,0:T(8,128)(2,1)}, u32[]{:S(2)}) copy-start(bf16[1,512,4608]{2,1,0:T(8,128)(2,1)} %all-gather.3.cloned.1.call-done) | copy-start | bytes 14155780
  105.2 3.0 %copy-start.10 = (bf16[1,4608,128]{2,1,0:T(8,128)(2,1)S(1)}, bf16[1,4608,128]{2,1,0:T(8,128)(2,1)}, u32[]{:S(2)}) copy-start(bf16[1,4608,128]{2,1,0:T(8,128)(2,1)} %param.20) | copy-start | bytes 3538948
  107.6 2.9 %collective-permute-start = (bf16[512,128]{0,1:T(8,128)(2,1)S(1)}, bf16[512,128]{0,1:T(8,128)(2,1)S(1)}, u32[]{:S(2)}, u32[]{:S(2)}) collective-permute-start(bf16[512,128]{0,1:T(8,128)(2,1)S(1)} %fusion.21), channel_id=1, source_target_pairs={{0,1},{1,0},{2,3},{3,2},{4,5},{5,4},{6,7},{7,6},{8,9},{9,8},{10,11... | collective-permute-start | bytes 393224 | tf_op jit(solution)/shard_map/ppermute | solution.py:27
  114.9 1.3 copy-start.4
  121.3 6.6 %copy-start.7 = (f32[1,4608]{1,0:T(1,128)S(1)}, f32[1,4608]{1,0:T(1,128)}, u32[]{:S(2)}) copy-start(f32[1,4608]{1,0:T(1,128)} %param.23) | copy-start | bytes 55300
  121.3 38.3 %all-to-all-start.1 = ((bf16[32,1,9217]{2,1,0:T(2,128)(2,1)}), bf16[32,1,9217]{2,1,0:T(2,128)(2,1)S(1)}, u32[]{:S(2)}, u32[]{:S(2)}) async-start(bf16[32,1,9217]{2,1,0:T(2,128)(2,1)} %copy.22), calls=%async_computation.1 | async-start | bytes 2392064 | tf_op jit(solution)/shard_map/all_to_all | solution.py:13
  159.8 0.8 copy-start.2
  165.4 49.3 %copy-start.5 = (f32[4608]{0:T(1024)S(1)}, f32[4608]{0:T(1024)}, u32[]{:S(2)}) copy-start(f32[4608]{0:T(1024)} %reduce.2) | copy-start | bytes 55300
Sparse Core Ops, SparseCore 0:
  37.7 63.6 all-gather.2
  115.0 98.4 reduce-scatter.1
where the time goes:
time: 225 us; the launch traced here: 223 us
  waiting for transfers between devices  155 us (69%)
  local copies, waits for them, and re-layouts  15.7 us (7%)
  between operations  15.6 us (7%)
  other arithmetic  15.2 us (7%)
  starting transfers between devices  13.4 us (6%)
  matrix products  7.99 us (4%)
    all_gather x1, waiting for transfers between devices, on_device(): block_rows = lax.all_gather(checked, 'dp', axis=0, tiled=True)  61.9 us
    reduce_scatter x1, waiting for transfers between devices, on_device(): lax.psum_scatter(jnp.dot(attended, w_output, preferred_element_type=jnp.f...  46.5 us
    all_to_all x1, waiting for transfers between devices, sent_together(): lax.all_to_all(both, axis, split_axis=split_dim, concat_axis=concat_dim,...  30.9 us
    all_to_all x1, waiting for transfers between devices, on_device(): lax.all_to_all(outgoing, 'section', split_axis=0, concat_axis=0, tiled=True)  16 us
    all_to_all x1, starting transfers between devices, sent_together(): lax.all_to_all(both, axis, split_axis=split_dim, concat_axis=concat_dim,...  6.55 us
    all_to_all x1, starting transfers between devices, on_device(): lax.all_to_all(outgoing, 'section', split_axis=0, concat_axis=0, tiled=True)  6.19 us
    reduce_sum x2, other arithmetic, rms_norm(): meansq = jnp.mean(values * values, axis=-1, keepdims=True)  4.54 us
  transfers between devices with their start and end apart: 5, of which 4 were waited for; matrix products, arithmetic and copies ran while one was open for 7% of the time, Pallas kernels for 0%

commit v1 on v0

v1 whole, which is shorter than its diff:
```python
import functools

import jax
import jax.numpy as jnp
import numpy as np
from jax import lax
from jax.experimental import pallas as pl
from jax.experimental.pallas import tpu as pltpu
from jax.sharding import PartitionSpec as P

MESH = pl.DeviceIdType.MESH
D = 4608
H = D // 2
HD = 128
NS = 8
NY = 4
NZ = 4
MB = 8
ROWS = 16
BLK = 32
EPS = 1e-06
F32 = jnp.float32
BF16 = jnp.bfloat16


def rotary_tables():
    freqs = (10000.0 ** (-2.0 * np.arange(HD // 2, dtype=np.float32) / HD)).astype(np.float32)
    angles = np.arange(512, dtype=np.float32)[:, None] * freqs[None, :]
    cosine, sine = np.cos(angles), np.sin(angles)
    full = np.stack(
        [np.concatenate([cosine, cosine], axis=1), np.concatenate([-sine, sine], axis=1)]
    )
    return full.astype(np.float32).reshape(2, NY, NZ, 32, HD)


def kernel(
    sec, blk, act_hbm, acc_hbm, loss_ref, gpre, wq_hbm, wkv_hbm, wo_hbm, gpost, tab,
    moved_hbm, newacc_hbm, check_hbm,
    act_v, asend, recv_a, moved_v, acc_v, bsend, b1, b2, b3, newacc_v,
    lsend, lry, lsum, lrz, lfin, lrc,
    nbuf, xh, wbuf, wobuf, rbuf, rrq, rrkv, qf, kf, vf, at2,
    pbuf, yrh, yrf, zrh, zrf, zs, fb, finr, outb, checkb,
    loc, a_s, a_r, bl_s, bl_r, cz_s, cz_r, cy_s, cy_r, cc_s, cc_r, dy_s, dy_r, dz_s, dz_r,
):
    s = lax.axis_index("section")
    d = lax.axis_index("dp")
    y = lax.div(d, 8)
    z = lax.rem(lax.div(d, 2), 4)
    c = lax.rem(d, 2)
    o = 1 - c

    def ring(v, r, n):
        return lax.rem(v + (r + n), n)

    def dp_of(yy, zz, cc):
        return (yy * NZ + zz) * 2 + cc

    at_y = {r: (s, dp_of(ring(y, r, NY), z, c)) for r in (1, 2, 3, -1)}
    at_z = {r: (s, dp_of(y, ring(z, r, NZ), c)) for r in (1, 2, 3, -1)}
    at_c = (s, dp_of(y, z, o))
    at_s = {r: (ring(s, r, NS), d) for r in range(1, NS)}

    barrier = pltpu.get_barrier_semaphore()
    greet = [at_s[r] for r in range(1, NS)] + [at_y[r] for r in (1, 2, 3)]
    greet += [at_z[r] for r in (1, 2, 3)] + [at_c]
    for who in greet:
        pl.semaphore_signal(barrier, inc=1, device_id=who, device_id_type=MESH)

    pending = []

    def remote(src, dst, send_sem, recv_sem, who):
        copy = pltpu.make_async_remote_copy(
            src_ref=src, dst_ref=dst, send_sem=send_sem, recv_sem=recv_sem,
            device_id=who, device_id_type=MESH,
        )
        copy.start()
        pending.append(copy)
        return copy

    load_act = pltpu.make_async_copy(act_hbm, act_v, loc.at[0])
    load_acc = pltpu.make_async_copy(acc_hbm, acc_v, loc.at[1])
    own_rows = pl.ds(pl.multiple_of(c * H, 128), H)
    own_lanes = pl.ds(pl.multiple_of(c * HD, 128), HD)
    kv_lanes = pl.ds(pl.multiple_of(2 * HD + c * HD, 128), HD)
    other_rows = pl.ds(pl.multiple_of(o * H, 128), H)
    load_wq = pltpu.make_async_copy(wq_hbm.at[own_rows, :], wbuf.at[:, own_lanes], loc.at[2])
    load_wkv = pltpu.make_async_copy(wkv_hbm.at[own_rows, :], wbuf.at[:, kv_lanes], loc.at[3])
    load_wo = pltpu.make_async_copy(wo_hbm.at[:, own_rows], wobuf.at[c], loc.at[4])
    load_act.start()
    load_acc.start()
    load_wq.start()
    load_wkv.start()
    load_wo.start()

    load_act.wait()
    for r in range(NS):
        to = ring(s, r, NS)
        at = jnp.int32(0)
        for j in range(MB):
            source = sec[to * MB + j]
            at = at + jnp.where((source >> 3) == s, source & 7, 0)
        if r == 0:
            recv_a[s] = act_v[at]
        else:
            asend[r] = act_v[at]
    lsend[...] = jnp.broadcast_to(loss_ref[...], (1, HD))

    pl.semaphore_wait(barrier, len(greet))

    from_s = [
        remote(asend.at[r], recv_a.at[s], a_s.at[r], a_r.at[r], at_s[r]) for r in range(1, NS)
    ]
    from_ly = [
        remote(lsend, lry.at[r], bl_s.at[8 + r], bl_r.at[8 + r], at_y[r]) for r in (1, 2, 3)
    ]
    w_q = remote(wq_hbm.at[other_rows, :], wbuf.at[:, own_lanes], cc_s.at[0], cc_r.at[0], at_c)
    w_kv = remote(wkv_hbm.at[other_rows, :], wbuf.at[:, kv_lanes], cc_s.at[1], cc_r.at[1], at_c)
    w_o = remote(wo_hbm.at[:, other_rows], wobuf.at[c], cc_s.at[2], cc_r.at[2], at_c)

    load_acc.wait()
    from_by = []
    for r in (1, 2, 3, 0):
        base = ring(y, r, NY) * 8

        def pick(k, carry, r=r, base=base):
            first = (base + k) * BLK
            at = jnp.int32(0)
            for b in range(BLK):
                source = blk[first + b]
                at = at + jnp.where((source >> 5) == d, source & 31, 0)
            into = b1.at[0] if r == 0 else bsend.at[r]
            into[lax.div(k, 2), lax.rem(k, 2)] = acc_v[at].astype(BF16)
            return carry

        lax.fori_loop(0, 8, pick, 0)
        if r:
            from_by.append(
                remote(bsend.at[r], b1.at[r], bl_s.at[r], bl_r.at[r], at_y[r])
            )

    for copy in from_s:
        copy.wait_recv()
    x = recv_a[sec[s * MB] >> 3]
    xf = x.astype(F32)
    meansq = jnp.mean(xf * xf, axis=-1, keepdims=True)
    normed = (xf * lax.rsqrt(meansq + EPS) * gpre[...]).astype(BF16)
    nbuf[0] = normed[:, :H]
    nbuf[1] = normed[:, H:]
    xh[y, z, c] = nbuf[c]
    core_n = remote(nbuf.at[o], xh.at[y, z, c], cc_s.at[3], cc_r.at[3], at_c)
    core_n.wait_recv()

    def gather_y(q, zz):
        return [
            remote(xh.at[y, zz], xh.at[y, zz], cy_s.at[q, 0], cy_r.at[q, 0], at_y[1]),
            remote(xh.at[y, zz], xh.at[y, zz], cy_s.at[q, 1], cy_r.at[q, 1], at_y[-1]),
        ]

    def pass_y(q, zz, copies):
        copies[0].wait_recv()
        low = xh.at[ring(y, -1, NY), zz, 0]
        first = remote(low, low, cy_s.at[q, 2], cy_r.at[q, 2], at_y[1])
        copies[1].wait_recv()
        high = xh.at[ring(y, 1, NY), zz, 1]
        return [first, remote(high, high, cy_s.at[q, 3], cy_r.at[q, 3], at_y[-1])]

    zp, zm, zf = ring(z, 1, NZ), ring(z, -1, NZ), ring(z, 2, NZ)
    order = [z, zm, zp, zf]
    near_z = [
        remote(xh.at[y, z], xh.at[y, z], cz_s.at[0], cz_r.at[0], at_z[1]),
        remote(xh.at[y, z], xh.at[y, z], cz_s.at[1], cz_r.at[1], at_z[-1]),
    ]
    near = [gather_y(0, z)]
    far = [pass_y(0, z, near[0])]
    near_z[0].wait_recv()
    far_z = [remote(xh.at[y, zm, 0], xh.at[y, zm, 0], cz_s.at[2], cz_r.at[2], at_z[1])]
    near.append(gather_y(1, zm))
    near_z[1].wait_recv()
    far_z.append(remote(xh.at[y, zp, 1], xh.at[y, zp, 1], cz_s.at[3], cz_r.at[3], at_z[-1]))
    near.append(gather_y(2, zp))

    for copy in from_ly:
        copy.wait_recv()
    lsum[...] = lsend[...] + lry[1] + lry[2] + lry[3]
    from_lz = [
        remote(lsum, lrz.at[r], bl_s.at[11 + r], bl_r.at[11 + r], at_z[r]) for r in (1, 2, 3)
    ]
    for copy in from_by:
        copy.wait_recv()
    from_bz = [
        remote(b1.at[:, ring(z, r, NZ)], b2.at[r], bl_s.at[3 + r], bl_r.at[3 + r], at_z[r])
        for r in (1, 2, 3)
    ]
    b2[0] = b1[:, z]

    far.append(pass_y(1, zm, near[1]))

    def project(q):
        zz = order[q]
        for copy in far[q]:
            copy.wait_recv()
        rows = xh[:, zz].reshape(128, H)
        res = jnp.dot(rows, wbuf[...], preferred_element_type=F32)
        for j in range(4):
            rbuf[q, j] = res[:, j * HD : (j + 1) * HD]
        return [
            remote(rbuf.at[q, o], rrq.at[q], cc_s.at[4 + q], cc_r.at[4 + q], at_c),
            remote(rbuf.at[q, pl.ds(2, 2)], rrkv.at[q], cc_s.at[8 + q], cc_r.at[8 + q], at_c),
        ]

    def finish(q, copies):
        zz = order[q]
        for copy in copies:
            copy.wait_recv()
        cosine = tab[0, :, zz].reshape(128, HD)
        sine = tab[1, :, zz].reshape(128, HD)
        query = rbuf[q, c] + rrq[q]
        key = rbuf[q, 2] + rrkv[q, 0]
        value = rbuf[q, 3] + rrkv[q, 1]
        query = query * cosine + pltpu.roll(query, HD // 2, 1) * sine
        key = key * cosine + pltpu.roll(key, HD // 2, 1) * sine
        qf[:, zz] = query.astype(BF16).reshape(NY, 32, HD)
        kf[:, zz] = key.astype(BF16).reshape(NY, 32, HD)
        vf[:, zz] = value.astype(BF16).reshape(NY, 32, HD)

    load_wq.wait()
    load_wkv.wait()
    w_q.wait_recv()
    w_kv.wait_recv()
    shared = [project(0)]
    for copy in far_z:
        copy.wait_recv()
    near.append(gather_y(3, zf))
    far.append(pass_y(2, zp, near[2]))
    for j in range(MB):
        moved_v[j] = recv_a[sec[s * MB + j] >> 3]
    store_moved = pltpu.make_async_copy(moved_v, moved_hbm, loc.at[5])
    store_moved.start()
    shared.append(project(1))
    finish(0, shared[0])
    far.append(pass_y(3, zf, near[3]))
    shared.append(project(2))
    finish(1, shared[1])
    shared.append(project(3))
    finish(2, shared[2])
    finish(3, shared[3])

    from_att = []
    for m in range(NY):
        keys = 128 * (m + 1)
        scores = lax.dot_general(
            qf[m].reshape(128, HD), kf[0 : m + 1].reshape(keys, HD),
            (((1,), (1,)), ((), ())), preferred_element_type=F32,
        ) * ((D / 32) ** (-0.5))
        capped = 50.0 * jnp.tanh(scores / 50.0)
        row = lax.broadcasted_iota(jnp.int32, (128, keys), 0) + 128 * m
        col = lax.broadcasted_iota(jnp.int32, (128, keys), 1)
        expd = jnp.where(col <= row, jnp.exp(capped), 0.0)
        total = jnp.sum(expd, axis=-1, keepdims=True)
        numer = jnp.dot(
            expd.astype(BF16), vf[0 : m + 1].reshape(keys, HD), preferred_element_type=F32
        )
        at2[c, m] = (numer / total).astype(BF16).reshape(NZ, 32, HD)
        from_att.append(
            remote(at2.at[c, m], at2.at[c, m], cc_s.at[12 + m], cc_r.at[12 + m], at_c)
        )

    load_wo.wait()
    w_o.wait_recv()
    for copy in from_att:
        copy.wait_recv()
    y1, y3, y2 = ring(y, 1, NY), ring(y, -1, NY), ring(y, 2, NY)
    back = [zf, zp, zm, z]
    halves, fulls = [], []

    def part(q):
        zz = back[q]
        first = at2[0, :, zz].reshape(128, HD)
        second = at2[1, :, zz].reshape(128, HD)
        res = jnp.dot(first, wobuf[0], preferred_element_type=F32)
        res = res + jnp.dot(second, wobuf[1], preferred_element_type=F32)
        pbuf[:, zz] = res.astype(BF16).reshape(NY, 2, ROWS, H)
        halves.append([
            remote(pbuf.at[y2, zz, 0], yrh.at[q, 0], dy_s.at[q, 0], dy_r.at[q, 0], at_y[1]),
            remote(pbuf.at[y2, zz, 1], yrh.at[q, 1], dy_s.at[q, 1], dy_r.at[q, 1], at_y[-1]),
        ])

    def middle(q):
        zz = back[q]
        halves[q][0].wait_recv()
        pbuf[y1, zz, 0] = (pbuf[y1, zz, 0].astype(F32) + yrh[q, 0].astype(F32)).astype(BF16)
        up = remote(pbuf.at[y1, zz], yrf.at[q, 0], dy_s.at[q, 2], dy_r.at[q, 2], at_y[1])
        halves[q][1].wait_recv()
        pbuf[y3, zz, 1] = (pbuf[y3, zz, 1].astype(F32) + yrh[q, 1].astype(F32)).astype(BF16)
        down = remote(pbuf.at[y3, zz], yrf.at[q, 1], dy_s.at[q, 3], dy_r.at[q, 3], at_y[-1])
        fulls.append([up, down])

    def reduced(q):
        for copy in fulls[q]:
            copy.wait_recv()
        return pbuf[y, back[q]].astype(F32) + yrf[q, 0].astype(F32) + yrf[q, 1].astype(F32)

    part(0)
    part(1)
    middle(0)
    part(2)
    middle(1)
    part(3)
    zs[0] = reduced(0).astype(BF16)
    z_half = [
        remote(zs.at[0, 0], zrh.at[0], dz_s.at[0], dz_r.at[0], at_z[1]),
        remote(zs.at[0, 1], zrh.at[1], dz_s.at[1], dz_r.at[1], at_z[-1]),
    ]
    middle(2)
    middle(3)

    for copy in from_bz + from_lz:
        copy.wait_recv()
    core_b = remote(b2.at[:, :, o], b3, bl_s.at[7], bl_r.at[7], at_c)
    lfin[...] = lsum[...] + lrz[1] + lrz[2] + lrz[3]
    core_l = remote(lfin, lrc, bl_s.at[15], bl_r.at[15], at_c)

    part_sum = reduced(1)
    z_half[0].wait_recv()
    zs[1, 0] = (part_sum[0] + zrh[0].astype(F32)).astype(BF16)
    zs[1, 1] = part_sum[1].astype(BF16)
    z_up = remote(zs.at[1], zrf.at[0], dz_s.at[2], dz_r.at[2], at_z[1])
    part_sum = reduced(2)
    z_half[1].wait_recv()
    zs[2, 0] = part_sum[0].astype(BF16)
    zs[2, 1] = (part_sum[1] + zrh[1].astype(F32)).astype(BF16)
    z_down = remote(zs.at[2], zrf.at[1], dz_s.at[3], dz_r.at[3], at_z[-1])

    core_l.wait_recv()
    core_b.wait_recv()
    factor = 32.0 / (lfin[...] + lrc[...])

    def place(b, carry):
        source = blk[d * BLK + b] >> 5
        ry = (y - (source >> 3)) & 3
        rz = (z - ((source >> 1) & 3)) & 3
        mine = b2[rz, ry, c].astype(F32)
        theirs = b3[rz, ry].astype(F32)
        newacc_v[b] = jnp.where((source & 1) == c, mine, theirs) * factor
        return carry

    lax.fori_loop(0, BLK, place, 0)
    store_acc = pltpu.make_async_copy(newacc_v, newacc_hbm, loc.at[6])
    store_acc.start()

    part_sum = reduced(3)
    z_up.wait_recv()
    z_down.wait_recv()
    fb[...] = part_sum + zrf[0].astype(F32) + zrf[1].astype(F32)
    last = remote(fb.at[o], finr, cc_s.at[16], cc_r.at[16], at_c)
    checked = recv_a[sec[s * MB] >> 3].astype(F32)
    last.wait_recv()
    mine = fb[c]
    theirs = finr[...]
    meansq = jnp.sum(mine * mine, axis=-1, keepdims=True)
    meansq = (meansq + jnp.sum(theirs * theirs, axis=-1, keepdims=True)) / D
    scale = lax.rsqrt(meansq + EPS)
    outb[c] = mine
    outb[o] = theirs
    for h in range(2):
        cols = slice(h * H, (h + 1) * H)
        checkb[h] = (checked[:, cols] + outb[h] * scale * gpost[:, cols]).astype(BF16)
    stores = [
        pltpu.make_async_copy(checkb.at[h], check_hbm.at[:, pl.ds(h * H, H)], loc.at[7 + h])
        for h in range(2)
    ]
    for copy in stores:
        copy.start()
    for copy in pending:
        copy.wait_send()
    for copy in [store_moved, store_acc] + stores:
        copy.wait()


def on_device(act, sec, acc, blk, loss, gpre, wq, wkv, wo, gpost):
    acc = acc.reshape(BLK, 2, D // HD, HD).transpose(0, 2, 1, 3).reshape(BLK, 72, HD)
    tab = jnp.asarray(rotary_tables())
    any_ = pl.BlockSpec(memory_space=pl.ANY)
    smem = pl.BlockSpec(memory_space=pltpu.SMEM)
    vmem = pl.BlockSpec(memory_space=pltpu.VMEM)
    V = pltpu.VMEM
    dma = pltpu.SemaphoreType.DMA
    moved, newacc, check = pl.pallas_call(
        kernel,
        out_shape=(
            jax.ShapeDtypeStruct((MB, ROWS, D), BF16),
            jax.ShapeDtypeStruct((BLK, 72, HD), F32),
            jax.ShapeDtypeStruct((ROWS, D), BF16),
        ),
        in_specs=[smem, smem, any_, any_, vmem, vmem, any_, any_, any_, vmem, vmem],
        out_specs=(any_, any_, any_),
        scratch_shapes=[
            V((MB, ROWS, D), BF16), V((NS, ROWS, D), BF16), V((NS, ROWS, D), BF16),
            V((MB, ROWS, D), BF16), V((BLK, 72, HD), F32),
            V((NY, NZ, 2, 72, HD), BF16), V((NY, NZ, 2, 72, HD), BF16),
            V((NZ, NY, 2, 72, HD), BF16), V((NZ, NY, 72, HD), BF16), V((BLK, 72, HD), F32),
            V((1, HD), F32), V((4, 1, HD), F32), V((1, HD), F32), V((4, 1, HD), F32),
            V((1, HD), F32), V((1, HD), F32),
            V((2, ROWS, H), BF16), V((NY, NZ, 2, ROWS, H), BF16), V((H, 4 * HD), BF16),
            V((2, HD, H), BF16), V((4, 4, 128, HD), F32), V((4, 128, HD), F32),
            V((4, 2, 128, HD), F32), V((NY, NZ, 32, HD), BF16), V((NY, NZ, 32, HD), BF16),
            V((NY, NZ, 32, HD), BF16), V((2, NY, NZ, 32, HD), BF16),
            V((NY, NZ, 2, ROWS, H), BF16), V((4, 2, ROWS, H), BF16),
            V((4, 2, 2, ROWS, H), BF16), V((2, ROWS, H), BF16), V((2, 2, ROWS, H), BF16),
            V((3, 2, ROWS, H), BF16), V((2, ROWS, H), F32), V((ROWS, H), F32),
            V((2, ROWS, H), F32), V((2, ROWS, H), BF16),
            dma((9,)), dma((NS,)), dma((NS,)), dma((16,)), dma((16,)), dma((4,)), dma((4,)),
            dma((4, 4)), dma((4, 4)), dma((17,)), dma((17,)), dma((4, 4)), dma((4, 4)),
            dma((4,)), dma((4,)),
        ],
        compiler_params=pltpu.CompilerParams(
            collective_id=0, has_side_effects=True, vmem_limit_bytes=60 * 1024 * 1024
        ),
        name="restore",
    )(sec, blk, act, acc, loss, gpre, wq[0], wkv[0], wo[0], gpost, tab)
    newacc = newacc.reshape(BLK, D // HD, 2, HD).transpose(0, 2, 1, 3).reshape(BLK, 2, D)
    return moved, newacc, check[None]


def solution(mesh):
    placed = (
        P("section", "dp", None),
        P(),
        P("dp", "section", None),
        P(),
        P("section", "dp"),
        P("section", None),
        P("section", None, "dp"),
        P("section", None, "dp"),
        P("section", "dp", None),
        P("section", None),
    )
    return jax.shard_map(
        on_device,
        mesh=mesh,
        in_specs=placed,
        out_specs=(P("section", "dp", None), P("dp", "section", None), P("section", "dp", None)),
        check_vma=False,
    )
```

time: 225 us -> 103 us (0.46)
  waiting for transfers between devices: 155 us -> 0 us
  Pallas kernels: 0 us -> 92.6 us
  other arithmetic: 15.2 us -> 0 us
  between operations: 15.6 us -> 1.31 us
  starting transfers between devices: 13.4 us -> 0 us
  matrix products: 7.99 us -> 0 us
  local copies, waits for them, and re-layouts: 15.7 us -> 8.99 us
    pallas_call x0 -> x1, Pallas kernels: none -> 92.6 us  [on_device(): pl.pallas_call(kernel, out_shape=(jax.ShapeDtypeStruct((MB, ROWS, D), BF1...]
    all_gather x1 -> x0, waiting for transfers between devices: 61.9 us -> none  [on_device(): block_rows = lax.all_gather(checked, 'dp', axis=0, tiled=True)]
    all_to_all x2 -> x0, waiting for transfers between devices: 46.9 us -> none  [the longest x1 30.9 us: sent_together(): lax.all_to_all(both, axis, split_axis=split_dim, concat_axis=concat_dim,...]
    reduce_scatter x1 -> x0, waiting for transfers between devices: 46.5 us -> none  [on_device(): lax.psum_scatter(jnp.dot(attended, w_output, preferred_element_type=jnp.f...]
    all_to_all x2 -> x0, starting transfers between devices: 12.7 us -> none  [the longest x1 6.55 us: sent_together(): lax.all_to_all(both, axis, split_axis=split_dim, concat_axis=concat_dim,...]
    dot_general x4 -> x0, matrix products: 7.99 us -> none  [the longest x1 3.93 us: on_device(): jnp.dot(attended, w_output, preferred_element_type=jnp.float32)]
    gather x6 -> x0, local copies, waits for them, and re-layouts: 7.45 us -> none  [the longest x1 1.89 us: on_device(): outgoing = jnp.take(activations, send_index, axis=0)]
    reduce_sum x5 -> x0, other arithmetic: 6.2 us -> none  [the longest x2 4.54 us: rms_norm(): meansq = jnp.mean(values * values, axis=-1, keepdims=True)]
  transfers between devices with their start and end apart: 5 -> 0, of which waited for: 4 -> 0; matrix products, arithmetic and copies ran while one was open for 7% -> 0% of each run, Pallas kernels for 0% -> 0%
where the time goes in v1:
time: 103 us
  Pallas kernels  92.6 us (90%)
  local copies, waits for them, and re-layouts  8.99 us (9%)
  between operations  1.31 us (1%)
    pallas_call x1, Pallas kernels, on_device(): pl.pallas_call(kernel, out_shape=(jax.ShapeDtypeStruct((MB, ROWS, D), BF1...  92.6 us
    unnamed x7, local copies, waits for them, and re-layouts  3.62 us
    reshape x1, local copies, waits for them, and re-layouts, on_device(): acc.reshape(BLK, 2, D // HD, HD).transpose(0, 2, 1, 3).reshape(BLK, 72, HD)  2.2 us

profile of v1, /device:TPU:1, one launch (start us, length us, event | category | flops | bytes accessed | tf_op | source)
XLA Modules:
  0.0 102.9 jit_solution(9180310851114095805)
XLA Ops:
  1.3 2.2 %reshape.22 = f32[32,2,36,128]{3,2,1,0:T(8,128)S(1)} reshape(f32[32,2,4608]{2,1,0:T(2,128)} %param.13) | data formatting | bytes 2359296 | tf_op jit(solution)/shard_map/reshape | solution.py:381
  3.5 1.6 %copy.17 = f32[32,36,2,128]{3,2,1,0:T(2,128)} copy(f32[32,36,2,128]{3,1,2,0:T(8,128)S(1)} %bitcast.14) | data formatting | bytes 2359296 | tf_op jit(solution)/shard_map/transpose | solution.py:381
  5.1 92.6 %restore.1 = (bf16[8,16,4608]{2,1,0:T(8,128)(2,1)}, f32[32,72,128]{2,1,0:T(8,128)}, bf16[16,4608]{1,0:T(8,128)(2,1)}) custom-call(s32[64]{0:T(128)} %sec.1, s32[1024]{0:T(1024)} %blk.1, bf16[8,16,4608]{2,1,0:T(8,128)(2,1)} %act_hbm.1, f32[32,72,128]{2,1,0:T(8,128)} %bitcast.15, f32[1,1]{1,0:T(1,128)S(6)} %copy.26.loss_ref, f32[1,4608]{1,0:T(1,128)} %gpre.1, ...), custom_call_target="tpu_custom_call" | custom-call | tf_op jit(solution)/shard_map/restore/pallas_call | solution.py:388
  97.7 1.4 %copy.23 = f32[32,36,2,128]{3,1,0,2:T(8,128)S(1)} copy(f32[32,36,2,128]{3,2,1,0:T(2,128)} %bitcast.16) | data formatting | bytes 2359296 | tf_op jit(solution)/shard_map/reshape | solution.py:421
  99.1 0.2 reshape.21
  99.2 0.0 copy-start
  99.3 1.9 %copy.19 = f32[32,2,4608]{2,1,0:T(2,128)} copy(f32[32,2,4608]{2,0,1:T(8,128)S(1)} %reshape.21) | data formatting | bytes 2359296
  101.2 0.0 copy-done
  101.2 0.0 copy-start.1
  101.2 1.0 copy.27
  102.2 0.0 copy-done.1
  102.2 0.7 copy.28
Async XLA Ops:
  99.2 1.9 %copy-start = (bf16[8,16,4608]{2,1,0:T(8,128)(2,1)S(1)}, bf16[8,16,4608]{2,1,0:T(8,128)(2,1)}, u32[]{:S(2)}) copy-start(bf16[8,16,4608]{2,1,0:T(8,128)(2,1)} %get-tuple-element.15) | copy-start | bytes 3538948
  101.2 1.0 %copy-start.1 = (bf16[16,4608]{1,0:T(8,128)(2,1)S(1)}, bf16[16,4608]{1,0:T(8,128)(2,1)}, u32[]{:S(2)}) copy-start(bf16[16,4608]{1,0:T(8,128)(2,1)} %get-tuple-element.8) | copy-start | bytes 442372

commit v2 on v1

v2 whole, which is shorter than its diff:
```python
import functools

import jax
import jax.numpy as jnp
import numpy as np
from jax import lax
from jax.experimental import pallas as pl
from jax.experimental.pallas import tpu as pltpu
from jax.sharding import PartitionSpec as P

MESH = pl.DeviceIdType.MESH
D = 4608
H = D // 2
HD = 128
NS = 8
NY = 4
NZ = 4
MB = 8
ROWS = 16
BLK = 32
EPS = 1e-06
F32 = jnp.float32
BF16 = jnp.bfloat16


def rotary_tables():
    freqs = (10000.0 ** (-2.0 * np.arange(HD // 2, dtype=np.float32) / HD)).astype(np.float32)
    angles = np.arange(512, dtype=np.float32)[:, None] * freqs[None, :]
    cosine, sine = np.cos(angles), np.sin(angles)
    full = np.stack(
        [np.concatenate([cosine, cosine], axis=1), np.concatenate([-sine, sine], axis=1)]
    )
    return full.astype(np.float32).reshape(2, NY, NZ, 32, HD)


def kernel(
    sec, blk, act_hbm, acc_hbm, loss_ref, gpre, wq_hbm, wkv_hbm, wo_hbm, gpost, tab,
    moved_hbm, newacc_hbm, check_hbm,
    act_v, asend, recv_a, moved_v, acc_v, bsend, b1, b2, b3, bre, newacc_v,
    lsend, lry, lsum, lrz, lfin, lrc,
    nbuf, xh, wbuf, wobuf, rbuf, rrq, rrkv, qf, kf, vf, at2,
    pbuf, yrh, yro, yrm, zrh, zro, zrm, zs, fb, finr, outb, checkb,
    loc, a_s, a_r, bl_s, bl_r, cz_s, cz_r, cy_s, cy_r, cc_s, cc_r, dy_s, dy_r, dz_s, dz_r, bz_s, bz_r,
):
    s = lax.axis_index("section")
    d = lax.axis_index("dp")
    y = lax.div(d, 8)
    z = lax.rem(lax.div(d, 2), 4)
    c = lax.rem(d, 2)
    o = 1 - c

    def ring(v, r, n):
        return lax.rem(v + (r + n), n)

    def dp_of(yy, zz, cc):
        return (yy * NZ + zz) * 2 + cc

    at_y = {r: (s, dp_of(ring(y, r, NY), z, c)) for r in (1, 2, 3, -1)}
    at_z = {r: (s, dp_of(y, ring(z, r, NZ), c)) for r in (1, 2, 3, -1)}
    at_c = (s, dp_of(y, z, o))
    ahead = 1 - 2 * c
    ya, yb, yf = ring(y, ahead, NY), ring(y, -ahead, NY), ring(y, 2, NY)
    za, zb, zf = ring(z, ahead, NZ), ring(z, -ahead, NZ), ring(z, 2, NZ)
    to_ya, to_yb = (s, dp_of(ya, z, c)), (s, dp_of(yb, z, c))
    to_za, to_zb = (s, dp_of(y, za, c)), (s, dp_of(y, zb, c))
    at_s = {r: (ring(s, r, NS), d) for r in range(1, NS)}

    barrier = pltpu.get_barrier_semaphore()
    greet = [at_s[r] for r in range(1, NS)] + [at_y[r] for r in (1, 2, 3)]
    greet += [at_z[r] for r in (1, 2, 3)] + [at_c]
    for who in greet:
        pl.semaphore_signal(barrier, inc=1, device_id=who, device_id_type=MESH)

    pending = []

    def remote(src, dst, send_sem, recv_sem, who):
        copy = pltpu.make_async_remote_copy(
            src_ref=src, dst_ref=dst, send_sem=send_sem, recv_sem=recv_sem,
            device_id=who, device_id_type=MESH,
        )
        copy.start()
        pending.append(copy)
        return copy

    load_act = pltpu.make_async_copy(act_hbm, act_v, loc.at[0])
    load_acc = pltpu.make_async_copy(acc_hbm, acc_v, loc.at[1])
    own_rows = pl.ds(pl.multiple_of(c * H, 128), H)
    own_lanes = pl.ds(pl.multiple_of(c * HD, 128), HD)
    kv_lanes = pl.ds(pl.multiple_of(2 * HD + c * HD, 128), HD)
    other_rows = pl.ds(pl.multiple_of(o * H, 128), H)
    load_wq = pltpu.make_async_copy(wq_hbm.at[own_rows, :], wbuf.at[:, own_lanes], loc.at[2])
    load_wkv = pltpu.make_async_copy(wkv_hbm.at[own_rows, :], wbuf.at[:, kv_lanes], loc.at[3])
    load_wo = pltpu.make_async_copy(wo_hbm.at[:, own_rows], wobuf.at[c], loc.at[4])
    load_act.start()
    load_acc.start()
    load_wq.start()
    load_wkv.start()
    load_wo.start()

    load_act.wait()
    for r in range(NS):
        to = ring(s, r, NS)
        at = jnp.int32(0)
        for j in range(MB):
            source = sec[to * MB + j]
            at = at + jnp.where((source >> 3) == s, source & 7, 0)
        if r == 0:
            recv_a[s] = act_v[at]
        else:
            asend[r] = act_v[at]
    lsend[...] = jnp.broadcast_to(loss_ref[...], (1, HD))

    pl.semaphore_wait(barrier, len(greet))

    from_s = [
        remote(asend.at[r], recv_a.at[s], a_s.at[r], a_r.at[r], at_s[r]) for r in range(1, NS)
    ]
    from_ly = [
        remote(lsend, lry.at[r], bl_s.at[8 + r], bl_r.at[8 + r], at_y[r]) for r in (1, 2, 3)
    ]
    w_q = remote(wq_hbm.at[other_rows, :], wbuf.at[:, own_lanes], cc_s.at[0], cc_r.at[0], at_c)
    w_kv = remote(wkv_hbm.at[other_rows, :], wbuf.at[:, kv_lanes], cc_s.at[1], cc_r.at[1], at_c)
    w_o = remote(wo_hbm.at[:, other_rows], wobuf.at[c], cc_s.at[2], cc_r.at[2], at_c)

    load_acc.wait()
    from_by = []
    for r in (1, 2, 3, 0):
        base = ring(y, r, NY) * 8

        def pick(k, carry, r=r, base=base):
            first = (base + k) * BLK
            at = jnp.int32(0)
            for b in range(BLK):
                source = blk[first + b]
                at = at + jnp.where((source >> 5) == d, source & 31, 0)
            into = b1.at[0] if r == 0 else bsend.at[r]
            into[lax.div(k, 2), lax.rem(k, 2)] = acc_v[at].astype(BF16)
            return carry

        lax.fori_loop(0, 8, pick, 0)
        if r:
            from_by.append(
                remote(bsend.at[r], b1.at[r], bl_s.at[r], bl_r.at[r], at_y[r])
            )

    for copy in from_s:
        copy.wait_recv()
    x = recv_a[sec[s * MB] >> 3]
    xf = x.astype(F32)
    meansq = jnp.mean(xf * xf, axis=-1, keepdims=True)
    normed = (xf * lax.rsqrt(meansq + EPS) * gpre[...]).astype(BF16)
    nbuf[0] = normed[:, :H]
    nbuf[1] = normed[:, H:]
    xh[y, z, c] = nbuf[c]
    core_n = remote(nbuf.at[o], xh.at[y, z, c], cc_s.at[3], cc_r.at[3], at_c)

    def gather_y(q, zz, h, i):
        piece = xh.at[y, zz, h]
        one = remote(piece, piece, cy_s.at[q, i, 0], cy_r.at[q, i, 0], to_ya)
        two = remote(piece, piece, cy_s.at[q, i, 1], cy_r.at[q, i, 1], to_yb)
        return [one, two]

    def gather_z(h, i):
        piece = xh.at[y, z, h]
        one = remote(piece, piece, cz_s.at[i, 0], cz_r.at[i, 0], to_za)
        two = remote(piece, piece, cz_s.at[i, 1], cz_r.at[i, 1], to_zb)
        return [one, two]

    def pass_y(q, zz, h, i):
        near[q, i][i].wait_recv()
        piece = xh.at[yb if i == 0 else ya, zz, h]
        far[q, i] = remote(
            piece, piece, cy_s.at[q, i, 2], cy_r.at[q, i, 2], to_ya if i == 0 else to_yb
        )

    def pass_z(i):
        zz, h = (zb, c) if i == 0 else (za, o)
        near_z[i][i].wait_recv()
        piece = xh.at[y, zz, h]
        far_z[i] = remote(
            piece, piece, cz_s.at[i, 2], cz_r.at[i, 2], to_za if i == 0 else to_zb
        )

    near, far, near_z, far_z = {}, {}, {}, {}
    order = [z, zb, za, zf]
    near_z[0] = gather_z(c, 0)
    near[0, 0] = gather_y(0, z, c, 0)
    core_n.wait_recv()
    near_z[1] = gather_z(o, 1)
    near[0, 1] = gather_y(0, z, o, 1)
    pass_y(0, z, c, 0)
    pass_z(0)
    near[1, 0] = gather_y(1, zb, c, 0)
    pass_y(0, z, o, 1)
    near_z[0][1].wait_recv()
    near[2, 0] = gather_y(2, za, c, 0)
    pass_z(1)
    near[2, 1] = gather_y(2, za, o, 1)
    near_z[1][0].wait_recv()
    near[1, 1] = gather_y(1, zb, o, 1)
    pass_y(1, zb, c, 0)
    pass_y(2, za, c, 0)

    def project(q):
        zz = order[q]
        near[q, 0][1].wait_recv()
        near[q, 1][0].wait_recv()
        far[q, 0].wait_recv()
        far[q, 1].wait_recv()
        rows = xh[:, zz].reshape(128, H)
        res = jnp.dot(rows, wbuf[...], preferred_element_type=F32)
        for j in range(4):
            rbuf[q, j] = res[:, j * HD : (j + 1) * HD]
        return [
            remote(rbuf.at[q, o], rrq.at[zz], cc_s.at[4 + zz], cc_r.at[4 + zz], at_c),
            remote(rbuf.at[q, pl.ds(2, 2)], rrkv.at[zz], cc_s.at[8 + zz], cc_r.at[8 + zz], at_c),
        ]

    def finish(q, copies):
        zz = order[q]
        for copy in copies:
            copy.wait_recv()
        cosine = tab[0, :, zz].reshape(128, HD)
        sine = tab[1, :, zz].reshape(128, HD)
        query = rbuf[q, c] + rrq[zz]
        key = rbuf[q, 2] + rrkv[zz, 0]
        value = rbuf[q, 3] + rrkv[zz, 1]
        query = query * cosine + pltpu.roll(query, HD // 2, 1) * sine
        key = key * cosine + pltpu.roll(key, HD // 2, 1) * sine
        qf[:, zz] = query.astype(BF16).reshape(NY, 32, HD)
        kf[:, zz] = key.astype(BF16).reshape(NY, 32, HD)
        vf[:, zz] = value.astype(BF16).reshape(NY, 32, HD)

    load_wq.wait()
    load_wkv.wait()
    w_q.wait_recv()
    w_kv.wait_recv()
    shared = {}
    shared[0] = project(0)
    pass_y(2, za, o, 1)
    pass_y(1, zb, o, 1)
    far_z[0].wait_recv()
    near[3, 0] = gather_y(3, zf, c, 0)
    far_z[1].wait_recv()
    near[3, 1] = gather_y(3, zf, o, 1)
    for copy in from_ly:
        copy.wait_recv()
    lsum[...] = lsend[...] + lry[1] + lry[2] + lry[3]
    from_lz = [
        remote(lsum, lrz.at[r], bl_s.at[11 + r], bl_r.at[11 + r], at_z[r]) for r in (1, 2, 3)
    ]
    for copy in from_by:
        copy.wait_recv()
    low, high = pl.ds(0, 2), pl.ds(2, 2)
    b_far = b1.at[:, ring(z, 2, NZ)]
    relay = [
        remote(b_far.at[low], bre.at[0], bz_s.at[0], bz_r.at[0], at_z[1]),
        remote(b_far.at[high], bre.at[1], bz_s.at[1], bz_r.at[1], at_z[-1]),
    ]
    from_bz = [
        remote(b1.at[:, ring(z, 1, NZ)], b2.at[1], bl_s.at[4], bl_r.at[4], at_z[1]),
        remote(b1.at[:, ring(z, 3, NZ)], b2.at[3], bl_s.at[6], bl_r.at[6], at_z[3]),
    ]
    b2[0] = b1[:, z]
    for j in range(MB):
        moved_v[j] = recv_a[sec[s * MB + j] >> 3]
    store_moved = pltpu.make_async_copy(moved_v, moved_hbm, loc.at[5])
    store_moved.start()
    shared[1] = project(1)
    finish(0, shared[0])
    pass_y(3, zf, c, 0)
    shared[2] = project(2)
    pass_y(3, zf, o, 1)
    finish(1, shared[1])
    finish(2, shared[2])
    relay[0].wait_recv()
    from_bz.append(
        remote(bre.at[0], b2.at[2, low], bz_s.at[2], bz_r.at[2], at_z[1])
    )
    relay[1].wait_recv()
    from_bz.append(
        remote(bre.at[1], b2.at[2, high], bz_s.at[3], bz_r.at[3], at_z[-1])
    )
    shared[3] = project(3)
    finish(3, shared[3])
    back = [zf, zb, za, z]
    keys, values = kf[...].reshape(512, HD), vf[...].reshape(512, HD)
    line = lax.broadcasted_iota(jnp.int32, (128, 512), 0)
    token = ((line >> 5) << 7) + (line & 31)
    col = lax.broadcasted_iota(jnp.int32, (128, 512), 1)
    from_att = []
    for m in range(4):
        scores = lax.dot_general(
            qf[:, back[m]].reshape(128, HD), keys,
            (((1,), (1,)), ((), ())), preferred_element_type=F32,
        ) * ((D / 32) ** (-0.5))
        capped = 50.0 * jnp.tanh(scores / 50.0)
        expd = jnp.where(col <= token + back[m] * 32, jnp.exp(capped), 0.0)
        total = jnp.sum(expd, axis=-1, keepdims=True)
        numer = jnp.dot(expd.astype(BF16), values, preferred_element_type=F32)
        zz = back[m]
        at2[c, zz] = (numer / total).astype(BF16)
        from_att.append(
            remote(at2.at[c, zz], at2.at[c, zz], cc_s.at[12 + zz], cc_r.at[12 + zz], at_c)
        )

    load_wo.wait()
    w_o.wait_recv()
    y_far, y_own, y_mid = {}, {}, {}

    def part(q):
        from_att[q].wait_recv()
        res = jnp.dot(at2[0, back[q]], wobuf[0], preferred_element_type=F32)
        res = res + jnp.dot(at2[1, back[q]], wobuf[1], preferred_element_type=F32)
        pbuf[:, back[q]] = res.astype(BF16).reshape(NY, 2, ROWS, H)

    def issue(q, i):
        zz, h = back[q], (c, o)[i]
        first, second = ((to_ya, to_yb), (to_yb, to_ya))[i]
        y_far[q, i] = remote(
            pbuf.at[yf, zz, h], yrh.at[q, i], dy_s.at[q, i, 0], dy_r.at[q, i, 0], first
        )
        y_own[q, i] = remote(
            pbuf.at[(yb, ya)[i], zz, h], yro.at[q, i], dy_s.at[q, i, 1], dy_r.at[q, i, 1], second
        )

    def middle(q, i):
        zz, h = back[q], (c, o)[i]
        next_y, who = ((ya, to_ya), (yb, to_yb))[i]
        y_far[q, i].wait_recv()
        total = pbuf[next_y, zz, h].astype(F32) + yrh[q, i].astype(F32)
        pbuf[next_y, zz, h] = total.astype(BF16)
        y_mid[q, i] = remote(
            pbuf.at[next_y, zz, h], yrm.at[q, i], dy_s.at[q, i, 2], dy_r.at[q, i, 2], who
        )

    def reduced(q, i):
        y_own[q, i].wait_recv()
        y_mid[q, i].wait_recv()
        total = pbuf[y, back[q], (c, o)[i]].astype(F32)
        return total + yro[q, i].astype(F32) + yrm[q, i].astype(F32)

    def send_z(value, kind, i, into, who):
        zs[kind, i] = value.astype(BF16)
        return remote(
            zs.at[kind, i], into.at[i], dz_s.at[kind, i], dz_r.at[kind, i], who
        )

    part(0)
    issue(0, 0)
    issue(0, 1)
    part(1)
    issue(1, 0)
    part(2)
    issue(2, 1)
    middle(0, 0)
    middle(0, 1)
    issue(2, 0)
    issue(1, 1)
    middle(1, 0)
    middle(2, 1)
    part(3)
    z_far = [send_z(reduced(0, 0), 0, 0, zrh, to_za)]
    z_far.append(send_z(reduced(0, 1), 0, 1, zrh, to_zb))
    issue(3, 0)
    issue(3, 1)
    middle(2, 0)
    middle(1, 1)
    z_own = [send_z(reduced(1, 0), 1, 0, zro, to_zb)]
    z_own.append(send_z(reduced(2, 1), 1, 1, zro, to_za))
    middle(3, 0)
    middle(3, 1)
    total = reduced(2, 0)
    z_far[0].wait_recv()
    z_mid = [send_z(total + zrh[0].astype(F32), 2, 0, zrm, to_za)]
    total = reduced(1, 1)
    z_far[1].wait_recv()
    z_mid.append(send_z(total + zrh[1].astype(F32), 2, 1, zrm, to_zb))

    for copy in from_bz + from_lz:
        copy.wait_recv()
    core_b = remote(b2.at[:, :, o], b3, bl_s.at[7], bl_r.at[7], at_c)
    lfin[...] = lsum[...] + lrz[1] + lrz[2] + lrz[3]
    core_l = remote(lfin, lrc, bl_s.at[15], bl_r.at[15], at_c)

    core_l.wait_recv()
    core_b.wait_recv()
    factor = 32.0 / (lfin[...] + lrc[...])[0, 0]

    def place(b, carry):
        source = blk[d * BLK + b] >> 5
        ry = (y - (source >> 3)) & 3
        rz = (z - ((source >> 1) & 3)) & 3
        mine = b2[rz, ry, c].astype(F32)
        theirs = b3[rz, ry].astype(F32)
        newacc_v[b] = jnp.where((source & 1) == c, mine, theirs) * factor
        return carry

    lax.fori_loop(0, BLK, place, 0)
    store_acc = pltpu.make_async_copy(newacc_v, newacc_hbm, loc.at[6])
    store_acc.start()

    sums = [reduced(3, 0), reduced(3, 1)]
    for i in range(2):
        z_own[i].wait_recv()
        z_mid[i].wait_recv()
        fb[i] = sums[i] + zro[i].astype(F32) + zrm[i].astype(F32)
    last = remote(fb.at[1], finr, cc_s.at[16], cc_r.at[16], at_c)
    checked = recv_a[sec[s * MB] >> 3].astype(F32)
    last.wait_recv()
    mine = fb[0]
    theirs = finr[...]
    meansq = jnp.sum(mine * mine, axis=-1, keepdims=True)
    meansq = (meansq + jnp.sum(theirs * theirs, axis=-1, keepdims=True)) / D
    scale = lax.rsqrt(meansq + EPS)
    outb[c] = mine
    outb[o] = theirs
    for h in range(2):
        cols = slice(h * H, (h + 1) * H)
        checkb[h] = (checked[:, cols] + outb[h] * scale * gpost[:, cols]).astype(BF16)
    stores = [
        pltpu.make_async_copy(checkb.at[h], check_hbm.at[:, pl.ds(h * H, H)], loc.at[7 + h])
        for h in range(2)
    ]
    for copy in stores:
        copy.start()
    for copy in pending:
        copy.wait_send()
    for copy in [store_moved, store_acc] + stores:
        copy.wait()


def on_device(act, sec, acc, blk, loss, gpre, wq, wkv, wo, gpost):
    tab = jnp.asarray(rotary_tables())
    any_ = pl.BlockSpec(memory_space=pl.ANY)
    smem = pl.BlockSpec(memory_space=pltpu.SMEM)
    vmem = pl.BlockSpec(memory_space=pltpu.VMEM)
    V = pltpu.VMEM
    dma = pltpu.SemaphoreType.DMA
    moved, newacc, check = pl.pallas_call(
        kernel,
        out_shape=(
            jax.ShapeDtypeStruct((MB, ROWS, D), BF16),
            jax.ShapeDtypeStruct((BLK, 2, D), F32),
            jax.ShapeDtypeStruct((ROWS, D), BF16),
        ),
        in_specs=[smem, smem, any_, any_, vmem, vmem, any_, any_, any_, vmem, vmem],
        out_specs=(any_, any_, any_),
        scratch_shapes=[
            V((MB, ROWS, D), BF16), V((NS, ROWS, D), BF16), V((NS, ROWS, D), BF16),
            V((MB, ROWS, D), BF16), V((BLK, 2, D), F32),
            V((NY, NZ, 2, 2, D), BF16), V((NY, NZ, 2, 2, D), BF16),
            V((NZ, NY, 2, 2, D), BF16), V((NZ, NY, 2, D), BF16), V((2, 2, 2, 2, D), BF16), V((BLK, 2, D), F32),
            V((1, HD), F32), V((4, 1, HD), F32), V((1, HD), F32), V((4, 1, HD), F32),
            V((1, HD), F32), V((1, HD), F32),
            V((2, ROWS, H), BF16), V((NY, NZ, 2, ROWS, H), BF16), V((H, 4 * HD), BF16),
            V((2, HD, H), BF16), V((4, 4, 128, HD), F32), V((4, 128, HD), F32),
            V((4, 2, 128, HD), F32), V((NY, NZ, 32, HD), BF16), V((NY, NZ, 32, HD), BF16),
            V((NY, NZ, 32, HD), BF16), V((2, 4, 128, HD), BF16),
            V((NY, NZ, 2, ROWS, H), BF16), V((4, 2, ROWS, H), BF16), V((4, 2, ROWS, H), BF16),
            V((4, 2, ROWS, H), BF16), V((2, ROWS, H), BF16), V((2, ROWS, H), BF16),
            V((2, ROWS, H), BF16), V((3, 2, ROWS, H), BF16), V((2, ROWS, H), F32),
            V((ROWS, H), F32), V((2, ROWS, H), F32), V((2, ROWS, H), BF16),
            dma((9,)), dma((NS,)), dma((NS,)), dma((16,)), dma((16,)), dma((2, 3)), dma((2, 3)),
            dma((4, 2, 3)), dma((4, 2, 3)), dma((17,)), dma((17,)),
            dma((4, 2, 3)), dma((4, 2, 3)), dma((3, 2)), dma((3, 2)), dma((4,)), dma((4,)),
        ],
        compiler_params=pltpu.CompilerParams(
            collective_id=0, has_side_effects=True, vmem_limit_bytes=60 * 1024 * 1024
        ),
        name="restore",
    )(sec, blk, act, acc, loss, gpre, wq[0], wkv[0], wo[0], gpost, tab)
    return moved, newacc, check[None]


def solution(mesh):
    placed = (
        P("section", "dp", None),
        P(),
        P("dp", "section", None),
        P(),
        P("section", "dp"),
        P("section", None),
        P("section", None, "dp"),
        P("section", None, "dp"),
        P("section", "dp", None),
        P("section", None),
    )
    return jax.shard_map(
        on_device,
        mesh=mesh,
        in_specs=placed,
        out_specs=(P("section", "dp", None), P("dp", "section", None), P("section", "dp", None)),
        check_vma=False,
    )
```

time: 103 us -> 89.7 us (0.87)
  Pallas kernels: 92.6 us -> 84.1 us
  local copies, waits for them, and re-layouts: 8.99 us -> 4.15 us
    pallas_call x1, Pallas kernels: 92.6 us -> 84.1 us  [on_device(): pl.pallas_call(kernel, out_shape=(jax.ShapeDtypeStruct((MB, ROWS, D), BF1...]
    reshape x3 -> x0, local copies, waits for them, and re-layouts: 3.75 us -> none  [the longest x1 2.2 us: on_device(): acc.reshape(BLK, 2, D // HD, HD).transpose(0, 2, 1, 3).reshape(BLK, 72, HD)]
    transpose x1 -> x0, local copies, waits for them, and re-layouts: 1.62 us -> none  [on_device(): acc.reshape(BLK, 2, D // HD, HD).transpose(0, 2, 1, 3).reshape(BLK, 72, HD)]
where the time goes in v2:
time: 89.7 us; the launch traced here: 89.5 us
  Pallas kernels  84.1 us (94%)
  local copies, waits for them, and re-layouts  4.15 us (5%)
  between operations  1.3 us (1%)
    pallas_call x1, Pallas kernels, on_device(): pl.pallas_call(kernel, out_shape=(jax.ShapeDtypeStruct((MB, ROWS, D), BF1...  84.1 us
    unnamed x7, local copies, waits for them, and re-layouts  4.15 us

profile of v2, /device:TPU:1, one launch (start us, length us, event | category | flops | bytes accessed | tf_op | source)
XLA Modules:
  0.0 89.5 jit_solution(4853108937834216342)
XLA Ops:
  1.3 84.1 %restore.1 = (bf16[8,16,4608]{2,1,0:T(8,128)(2,1)}, f32[32,2,4608]{2,1,0:T(2,128)}, bf16[16,4608]{1,0:T(8,128)(2,1)}) custom-call(s32[64]{0:T(128)} %sec.1, s32[1024]{0:T(1024)} %blk.1, bf16[8,16,4608]{2,1,0:T(8,128)(2,1)} %act_hbm.1, f32[32,2,4608]{2,1,0:T(2,128)} %acc_hbm.1, f32[1,1]{1,0:T(1,128)S(6)} %copy.17.loss_ref, f32[1,4608]{1,0:T(1,128)} %gpre.1, ...), custom_call_target="tpu_custom_call" | custom-call | tf_op jit(solution)/shard_map/restore/pallas_call | solution.py:440
  85.4 0.0 copy-start
  85.4 2.5 %copy.18 = bf16[8,16,4608]{2,1,0:T(8,128)(2,1)} copy(bf16[8,16,4608]{2,1,0:T(8,128)(2,1)} %get-tuple-element.12) | data formatting | bytes 2359296
  87.9 0.0 copy-done
  87.9 0.0 copy-start.1
  87.9 1.0 %copy.19 = f32[32,2,4608]{2,1,0:T(2,128)} copy(f32[32,2,4608]{2,1,0:T(2,128)S(1)} %copy-done) | data formatting | bytes 2359296
  88.9 0.0 copy-done.1
  88.9 0.7 copy.20
Async XLA Ops:
  85.4 2.5 %copy-start = (f32[32,2,4608]{2,1,0:T(2,128)S(1)}, f32[32,2,4608]{2,1,0:T(2,128)}, u32[]{:S(2)}) copy-start(f32[32,2,4608]{2,1,0:T(2,128)} %get-tuple-element.13) | copy-start | bytes 3538948
  87.9 1.0 %copy-start.1 = (bf16[16,4608]{1,0:T(8,128)(2,1)S(1)}, bf16[16,4608]{1,0:T(8,128)(2,1)}, u32[]{:S(2)}) copy-start(bf16[16,4608]{1,0:T(8,128)(2,1)} %get-tuple-element.8) | copy-start | bytes 442372

commit v3 on v2

v3 whole, which is shorter than its diff:
```python
import functools

import jax
import jax.numpy as jnp
import numpy as np
from jax import lax
from jax.experimental import pallas as pl
from jax.experimental.pallas import tpu as pltpu
from jax.sharding import PartitionSpec as P

MESH = pl.DeviceIdType.MESH
D = 4608
H = D // 2
HD = 128
NS = 8
NY = 4
NZ = 4
MB = 8
ROWS = 16
BLK = 32
EPS = 1e-06
NP = 2
HP = H // NP
F32 = jnp.float32
BF16 = jnp.bfloat16

GATHER = (
    ("near", 0, 1), ("row", 0, 0, 1), ("row", 0, 0, 0), ("near", 0, 0), ("near", 1, 1),
    ("row", 0, 1, 0), ("row", 0, 1, 1), ("near", 1, 0), ("ony", 0, 0, 1), ("ony", 0, 0, 0),
    ("row", 1, 0, 1), ("ony", 0, 1, 0), ("ony", 0, 1, 1), ("row", 2, 0, 1), ("row", 1, 0, 0),
    ("row", 2, 0, 0), ("onz", 0, 0), ("onz", 0, 1), ("row", 2, 1, 1), ("row", 1, 1, 1),
    ("moved",), ("onz", 1, 1), ("onz", 1, 0), ("ony", 2, 0, 1), ("project", 0), ("row", 1, 1, 0),
    ("ony", 1, 0, 1), ("row", 2, 1, 0), ("blocks",), ("row", 3, 1, 1), ("ony", 1, 0, 0),
    ("ony", 1, 1, 1), ("ony", 1, 1, 0), ("ony", 2, 1, 1), ("row", 3, 1, 0), ("ony", 2, 1, 0),
    ("row", 3, 0, 0), ("row", 3, 0, 1), ("ony", 2, 0, 0), ("ony", 3, 1, 1), ("ony", 3, 1, 0),
    ("relay",), ("ony", 3, 0, 0), ("ony", 3, 0, 1), ("project", 1), ("finish", 0), ("project", 2),
    ("project", 3), ("finish", 1), ("finish", 2), ("finish", 3),
)

REDUCE = (
    ("part", 0), ("far", 0, 0, 0), ("far", 0, 0, 1), ("part", 1), ("far", 1, 0, 0),
    ("side", 1, 1, 0), ("side", 1, 0, 0), ("attend", 3), ("own", 0, 0, 0), ("side", 1, 0, 1),
    ("side", 1, 1, 1), ("far", 0, 1, 0), ("far", 1, 1, 0), ("far", 0, 1, 1), ("middle", 0, 0, 0),
    ("far", 1, 0, 1), ("part", 2), ("own", 0, 1, 1), ("far", 2, 0, 0), ("own", 0, 1, 0),
    ("side", 2, 1, 0), ("side", 2, 1, 1), ("middle", 0, 1, 0), ("own", 0, 0, 1), ("part", 3),
    ("middle", 0, 0, 1), ("side", 2, 0, 1), ("zfar", 0, 0), ("cores",), ("middle", 0, 1, 1),
    ("side", 2, 0, 0), ("far", 2, 1, 1), ("middle", 2, 0, 0), ("middle", 1, 0, 0), ("zfar", 1, 0),
    ("far", 1, 1, 1), ("middle", 1, 0, 1), ("zfar", 0, 1), ("far", 2, 1, 0), ("middle", 1, 1, 0),
    ("zfar", 1, 1), ("middle", 2, 1, 1), ("far", 2, 0, 1), ("far", 3, 1, 1), ("far", 3, 0, 0),
    ("zmid", 0, 0), ("zown", 0, 0), ("middle", 1, 1, 1), ("middle", 2, 1, 0), ("far", 3, 1, 0),
    ("own", 3, 0, 0), ("zown", 0, 1), ("zmid", 1, 0), ("middle", 2, 0, 1), ("far", 3, 0, 1),
    ("zown", 1, 1), ("middle", 3, 0, 0), ("own", 3, 1, 1), ("own", 3, 1, 0), ("zmid", 1, 1),
    ("place",), ("middle", 3, 1, 0), ("middle", 3, 1, 1), ("zown", 1, 0), ("own", 3, 0, 1),
    ("zmid", 0, 1), ("middle", 3, 0, 1), ("finish", 1, 1), ("finish", 0, 0), ("finish", 1, 0),
    ("finish", 0, 1),
)


def rotary_tables():
    freqs = (10000.0 ** (-2.0 * np.arange(HD // 2, dtype=np.float32) / HD)).astype(np.float32)
    angles = np.arange(512, dtype=np.float32)[:, None] * freqs[None, :]
    cosine, sine = np.cos(angles), np.sin(angles)
    full = np.stack(
        [np.concatenate([cosine, cosine], axis=1), np.concatenate([-sine, sine], axis=1)]
    )
    return full.astype(np.float32).reshape(2, NY, NZ, 32, HD)


def kernel(
    sec_hbm, blk_hbm, act_hbm, acc_hbm, loss_hbm, gpre_hbm, wq_hbm, wkv_hbm, wo_hbm, gpost_hbm, tab_hbm,
    moved_v, newacc_v, checkb,
    act_v, asend, recv_a, acc_v, bsend, b1, b2, b3, bre,
    lsend, lry, lsum, lrz, lfin, lrc,
    nbuf, xh, wbuf, wobuf, rbuf, rrq, rrkv, qf, kf, vf, at2,
    pbuf, yrh, yro, yrm, zrh, zro, zrm, zs, fb, finr, outb, tab, sec, blk, loss_ref, gpre, gpost,
    zrs, loc, df_s, df_r, dx_s, dx_r, a_s, a_r, bl_s, bl_r, cz_s, cz_r, cy_s, cy_r, cc_s, cc_r, dy_s, dy_r, dz_s, dz_r, bz_s, bz_r,
):
    s = lax.axis_index("section")
    d = lax.axis_index("dp")
    y = lax.div(d, 8)
    z = lax.rem(lax.div(d, 2), 4)
    c = lax.rem(d, 2)
    o = 1 - c

    def ring(v, r, n):
        return lax.rem(v + (r + n), n)

    def dp_of(yy, zz, cc):
        return (yy * NZ + zz) * 2 + cc

    at_y = {r: (s, dp_of(ring(y, r, NY), z, c)) for r in (1, 2, 3, -1)}
    at_z = {r: (s, dp_of(y, ring(z, r, NZ), c)) for r in (1, 2, 3, -1)}
    at_c = (s, dp_of(y, z, o))
    ahead = 1 - 2 * c
    ya, yb, yf = ring(y, ahead, NY), ring(y, -ahead, NY), ring(y, 2, NY)
    za, zb, zf = ring(z, ahead, NZ), ring(z, -ahead, NZ), ring(z, 2, NZ)
    to_ya, to_yb = (s, dp_of(ya, z, c)), (s, dp_of(yb, z, c))
    to_za, to_zb = (s, dp_of(y, za, c)), (s, dp_of(y, zb, c))
    at_s = {r: (ring(s, r, NS), d) for r in range(1, NS)}

    barrier = pltpu.get_barrier_semaphore()
    greet = [at_s[r] for r in range(1, NS)] + [at_y[r] for r in (1, 2, 3)]
    greet += [at_z[r] for r in (1, 2, 3)] + [at_c]
    for who in greet:
        pl.semaphore_signal(barrier, inc=1, device_id=who, device_id_type=MESH)

    pending, seen = [], set()

    def arrived(copy):
        if id(copy) not in seen:
            seen.add(id(copy))
            copy.wait_recv()

    def remote(src, dst, send_sem, recv_sem, who):
        copy = pltpu.make_async_remote_copy(
            src_ref=src, dst_ref=dst, send_sem=send_sem, recv_sem=recv_sem,
            device_id=who, device_id_type=MESH,
        )
        copy.start()
        pending.append(copy)
        return copy

    load_act = pltpu.make_async_copy(act_hbm, act_v, loc.at[0])
    load_acc = pltpu.make_async_copy(acc_hbm, acc_v, loc.at[1])
    own_rows = pl.ds(pl.multiple_of(c * H, 128), H)
    own_lanes = pl.ds(pl.multiple_of(c * HD, 128), HD)
    kv_lanes = pl.ds(pl.multiple_of(2 * HD + c * HD, 128), HD)
    other_rows = pl.ds(pl.multiple_of(o * H, 128), H)
    load_wq = pltpu.make_async_copy(wq_hbm.at[own_rows, :], wbuf.at[:, own_lanes], loc.at[2])
    load_wkv = pltpu.make_async_copy(wkv_hbm.at[own_rows, :], wbuf.at[:, kv_lanes], loc.at[3])
    load_wo = pltpu.make_async_copy(wo_hbm.at[:, own_rows], wobuf.at[c], loc.at[4])
    load_tab = pltpu.make_async_copy(tab_hbm, tab, loc.at[9])
    small = [
        pltpu.make_async_copy(source, into, loc.at[10 + i])
        for i, (source, into) in enumerate(
            ((sec_hbm, sec), (loss_hbm, loss_ref), (blk_hbm, blk), (gpre_hbm, gpre),
             (gpost_hbm, gpost))
        )
    ]
    load_act.start()
    for copy in small:
        copy.start()
    load_acc.start()
    load_wq.start()
    load_wkv.start()
    load_wo.start()
    load_tab.start()

    load_act.wait()
    small[0].wait()
    small[1].wait()
    for r in range(NS):
        to = ring(s, r, NS)
        at = jnp.int32(0)
        for j in range(MB):
            source = sec[to * MB + j]
            at = at + jnp.where((source >> 3) == s, source & 7, 0)
        if r == 0:
            recv_a[s] = act_v[at]
        else:
            asend[r] = act_v[at]
    lsend[...] = jnp.broadcast_to(loss_ref[...], (1, HD))

    pl.semaphore_wait(barrier, len(greet))

    from_s = [
        remote(asend.at[r], recv_a.at[s], a_s.at[r], a_r.at[r], at_s[r]) for r in range(1, NS)
    ]
    from_ly = [
        remote(lsend, lry.at[r], bl_s.at[8 + r], bl_r.at[8 + r], at_y[r]) for r in (1, 2, 3)
    ]
    w_q = remote(wq_hbm.at[other_rows, :], wbuf.at[:, own_lanes], cc_s.at[0], cc_r.at[0], at_c)
    w_kv = remote(wkv_hbm.at[other_rows, :], wbuf.at[:, kv_lanes], cc_s.at[1], cc_r.at[1], at_c)
    w_o = remote(wo_hbm.at[:, other_rows], wobuf.at[c], cc_s.at[2], cc_r.at[2], at_c)

    load_acc.wait()
    for copy in small[2:]:
        copy.wait()
    from_by = []
    for r in (1, 2, 3, 0):
        base = ring(y, r, NY) * 8

        def pick(k, carry, r=r, base=base):
            first = (base + k) * BLK
            at = jnp.int32(0)
            for b in range(BLK):
                source = blk[first + b]
                at = at + jnp.where((source >> 5) == d, source & 31, 0)
            into = b1.at[0] if r == 0 else bsend.at[r]
            into[lax.div(k, 2), lax.rem(k, 2)] = acc_v[at].astype(BF16)
            return carry

        lax.fori_loop(0, 8, pick, 0)
        if r:
            from_by.append(
                remote(bsend.at[r], b1.at[r], bl_s.at[r], bl_r.at[r], at_y[r])
            )

    for copy in from_s:
        copy.wait_recv()
    x = recv_a[sec[s * MB] >> 3]
    xf = x.astype(F32)
    meansq = jnp.mean(xf * xf, axis=-1, keepdims=True)
    normed = (xf * lax.rsqrt(meansq + EPS) * gpre[...]).astype(BF16)
    nbuf[0] = normed[:, :H]
    nbuf[1] = normed[:, H:]
    xh[y, z, c] = nbuf[c]
    core_n = remote(nbuf.at[o], xh.at[y, z, c], cc_s.at[3], cc_r.at[3], at_c)

    half = (c, o)

    def piece_of(yy, zz, i, p):
        return xh.at[yy, zz, half[i], :, pl.ds(p * HP, HP)]

    order = [z, zb, za, zf]
    near_z, far_z, rows_y, rows_on = {}, {}, {}, {}

    def do_near(i, p):
        piece = piece_of(y, z, i, p)
        for way, who in enumerate((to_za, to_zb)):
            near_z[i, p, way] = remote(
                piece, piece, cz_s.at[i, way, p], cz_r.at[i, way, p], who
            )

    def do_row(q, i, p):
        if q == 1 or q == 2:
            arrived(near_z[i, p, q - 1])
        if q == 3:
            far_z[i, p].wait_recv()
        piece = piece_of(y, order[q], i, p)
        for way, who in enumerate((to_ya, to_yb)):
            rows_y[q, i, p, way] = remote(
                piece, piece, cy_s.at[q, i, way, p], cy_r.at[q, i, way, p], who
            )

    def do_onz(i, p):
        arrived(near_z[i, p, i])
        piece = piece_of(y, (zb, za)[i], i, p)
        far_z[i, p] = remote(
            piece, piece, cz_s.at[i, 2, p], cz_r.at[i, 2, p], (to_za, to_zb)[i]
        )

    def do_ony(q, i, p):
        rows_y[q, i, p, i].wait_recv()
        piece = piece_of((yb, ya)[i], order[q], i, p)
        rows_on[q, i, p] = remote(
            piece, piece, cy_s.at[q, i, 2, p], cy_r.at[q, i, 2, p], (to_ya, to_yb)[i]
        )

    def do_project(q):
        if q == 0:
            load_tab.wait()
            load_wq.wait()
            load_wkv.wait()
            w_q.wait_recv()
            w_kv.wait_recv()
        zz = order[q]
        for i in range(2):
            for p in range(NP):
                rows_y[q, i, p, 1 - i].wait_recv()
                rows_on[q, i, p].wait_recv()
        rows = xh[:, zz].reshape(128, H)
        res = jnp.dot(rows, wbuf[...], preferred_element_type=F32)
        for j in range(4):
            rbuf[q, j] = res[:, j * HD : (j + 1) * HD]
        shared[q] = [
            remote(rbuf.at[q, o], rrq.at[zz], cc_s.at[4 + zz], cc_r.at[4 + zz], at_c),
            remote(rbuf.at[q, pl.ds(2, 2)], rrkv.at[zz], cc_s.at[8 + zz], cc_r.at[8 + zz], at_c),
        ]

    def do_finish(q):
        zz = order[q]
        for copy in shared[q]:
            copy.wait_recv()
        cosine = tab[0, :, zz].reshape(128, HD)
        sine = tab[1, :, zz].reshape(128, HD)
        query = rbuf[q, c] + rrq[zz]
        key = rbuf[q, 2] + rrkv[zz, 0]
        value = rbuf[q, 3] + rrkv[zz, 1]
        query = query * cosine + pltpu.roll(query, HD // 2, 1) * sine
        key = key * cosine + pltpu.roll(key, HD // 2, 1) * sine
        qf[:, zz] = query.astype(BF16).reshape(NY, 32, HD)
        kf[:, zz] = key.astype(BF16).reshape(NY, 32, HD)
        vf[:, zz] = value.astype(BF16).reshape(NY, 32, HD)

    shared, relay, from_lz, from_bz = {}, [], [], []
    low, high = pl.ds(0, 2), pl.ds(2, 2)

    def do_blocks():
        for copy in from_ly:
            copy.wait_recv()
        lsum[...] = lsend[...] + lry[1] + lry[2] + lry[3]
        from_lz.extend(
            remote(lsum, lrz.at[r], bl_s.at[11 + r], bl_r.at[11 + r], at_z[r])
            for r in (1, 2, 3)
        )
        for copy in from_by:
            copy.wait_recv()
        b_far = b1.at[:, ring(z, 2, NZ)]
        relay.append(remote(b_far.at[low], bre.at[0], bz_s.at[0], bz_r.at[0], at_z[1]))
        relay.append(remote(b_far.at[high], bre.at[1], bz_s.at[1], bz_r.at[1], at_z[-1]))
        for r in (1, 3):
            from_bz.append(
                remote(b1.at[:, ring(z, r, NZ)], b2.at[r], bl_s.at[3 + r], bl_r.at[3 + r], at_z[r])
            )
        b2[0] = b1[:, z]

    def do_relay():
        for i, (part_of, who) in enumerate(((low, at_z[1]), (high, at_z[-1]))):
            relay[i].wait_recv()
            from_bz.append(
                remote(bre.at[i], b2.at[2, part_of], bz_s.at[2 + i], bz_r.at[2 + i], who)
            )

    def do_moved():
        for j in range(MB):
            moved_v[j] = recv_a[sec[s * MB + j] >> 3]

    steps = dict(
        near=do_near, row=do_row, onz=do_onz, ony=do_ony, project=do_project,
        finish=do_finish, blocks=do_blocks, relay=do_relay, moved=do_moved,
    )
    waited = False
    for name, *which in GATHER:
        second = (name == "near" and which[0] == 1) or (name == "row" and which[:2] == [0, 1])
        if second and not waited:
            core_n.wait_recv()
            waited = True
        with jax.named_scope("_".join([name] + [str(w) for w in which])):
            steps[name](*which)
    back = [zf, zb, za, z]
    keys, values = kf[...].reshape(512, HD), vf[...].reshape(512, HD)
    line = lax.broadcasted_iota(jnp.int32, (128, 512), 0)
    token = ((line >> 5) << 7) + (line & 31)
    col = lax.broadcasted_iota(jnp.int32, (128, 512), 1)
    from_att = {}

    def do_attend(m):
        scores = lax.dot_general(
            qf[:, back[m]].reshape(128, HD), keys,
            (((1,), (1,)), ((), ())), preferred_element_type=F32,
        ) * ((D / 32) ** (-0.5))
        capped = 50.0 * jnp.tanh(scores / 50.0)
        expd = jnp.where(col <= token + back[m] * 32, jnp.exp(capped), 0.0)
        total = jnp.sum(expd, axis=-1, keepdims=True)
        numer = jnp.dot(expd.astype(BF16), values, preferred_element_type=F32)
        zz = back[m]
        at2[c, zz] = (numer / total).astype(BF16)
        from_att[m] = remote(
            at2.at[c, zz], at2.at[c, zz], cc_s.at[12 + zz], cc_r.at[12 + zz], at_c
        )

    for m in range(3):
        do_attend(m)

    y_far, y_own, y_mid, z_side, z_far, z_own, z_mid, late = {}, {}, {}, {}, {}, {}, {}, {}

    def cols(p):
        return pl.ds(p * HP, HP)

    def mine_at(yy, q, i, p):
        return pbuf.at[yy, back[q], half[i], :, cols(p)]

    def do_part(q):
        if q == 0:
            load_wo.wait()
            w_o.wait_recv()
        from_att[q].wait_recv()
        res = jnp.dot(at2[0, back[q]], wobuf[0], preferred_element_type=F32)
        res = res + jnp.dot(at2[1, back[q]], wobuf[1], preferred_element_type=F32)
        pbuf[:, back[q]] = res.astype(BF16).reshape(NY, 2, ROWS, H)

    def do_far(q, i, p):
        y_far[q, i, p] = remote(
            mine_at(yf, q, i, p), yrh.at[q, i, :, cols(p)],
            dy_s.at[q, i, 0, p], dy_r.at[q, i, 0, p], (to_ya, to_yb)[i],
        )

    def do_own(q, i, p):
        source = mine_at((yb, ya)[i], q, i, p)
        if q == 3:
            z_side[1, i, p].wait_recv()
            z_side[2, i, p].wait_recv()
            total = source[...].astype(F32) + zrs[0, i, :, cols(p)].astype(F32)
            source[...] = (total + zrs[1, i, :, cols(p)].astype(F32)).astype(BF16)
        y_own[q, i, p] = remote(
            source, yro.at[q, i, :, cols(p)],
            dy_s.at[q, i, 1, p], dy_r.at[q, i, 1, p], (to_yb, to_ya)[i],
        )

    def do_side(q, i, p):
        z_side[q, i, p] = remote(
            mine_at((yb, ya)[i], q, i, p), zrs.at[q - 1, i, :, cols(p)],
            dx_s.at[q - 1, i, p], dx_r.at[q - 1, i, p], (to_zb, to_za)[q - 1],
        )

    def do_middle(q, i, p):
        y_far[q, i, p].wait_recv()
        source = mine_at((ya, yb)[i], q, i, p)
        total = source[...].astype(F32) + yrh[q, i, :, cols(p)].astype(F32)
        source[...] = total.astype(BF16)
        y_mid[q, i, p] = remote(
            source, yrm.at[q, i, :, cols(p)],
            dy_s.at[q, i, 2, p], dy_r.at[q, i, 2, p], (to_ya, to_yb)[i],
        )

    def reduced(q, i, p):
        total = mine_at(y, q, i, p)[...].astype(F32)
        if q == 0 or q == 3:
            y_own[q, i, p].wait_recv()
            total = total + yro[q, i, :, cols(p)].astype(F32)
        y_mid[q, i, p].wait_recv()
        return total + yrm[q, i, :, cols(p)].astype(F32)

    def send_z(value, kind, i, p, into, who):
        zs[kind, i, :, cols(p)] = value.astype(BF16)
        return remote(
            zs.at[kind, i, :, cols(p)], into.at[i, :, cols(p)],
            dz_s.at[kind, i, p], dz_r.at[kind, i, p], who,
        )

    def do_zfar(i, p):
        z_far[i, p] = send_z(reduced(0, i, p), 0, i, p, zrh, (to_za, to_zb)[i])

    def do_zown(i, p):
        z_own[i, p] = send_z(reduced(1 + i, i, p), 1, i, p, zro, (to_zb, to_za)[i])

    def do_zmid(i, p):
        total = reduced(2 - i, i, p)
        z_far[i, p].wait_recv()
        total = total + zrh[i, :, cols(p)].astype(F32)
        z_mid[i, p] = send_z(total, 2, i, p, zrm, (to_za, to_zb)[i])

    def do_cores():
        for copy in from_bz + from_lz:
            copy.wait_recv()
        late["blocks"] = remote(b2.at[:, :, o], b3, bl_s.at[7], bl_r.at[7], at_c)
        lfin[...] = lsum[...] + lrz[1] + lrz[2] + lrz[3]
        late["loss"] = remote(lfin, lrc, bl_s.at[15], bl_r.at[15], at_c)

    def do_place():
        late["loss"].wait_recv()
        late["blocks"].wait_recv()
        factor = 32.0 / (lfin[...] + lrc[...])[0, 0]

        def place(b, carry):
            source = blk[d * BLK + b] >> 5
            ry = (y - (source >> 3)) & 3
            rz = (z - ((source >> 1) & 3)) & 3
            mine = b2[rz, ry, c].astype(F32)
            theirs = b3[rz, ry].astype(F32)
            newacc_v[b] = jnp.where((source & 1) == c, mine, theirs) * factor
            return carry

        lax.fori_loop(0, BLK, place, 0)

    def do_finish_sum(i, p):
        total = reduced(3, i, p)
        z_own[i, p].wait_recv()
        z_mid[i, p].wait_recv()
        total = total + zro[i, :, cols(p)].astype(F32)
        fb[i, :, cols(p)] = total + zrm[i, :, cols(p)].astype(F32)
        if i == 1:
            late[p] = remote(
                fb.at[1, :, cols(p)], finr.at[:, cols(p)], df_s.at[p], df_r.at[p], at_c
            )

    steps = dict(
        part=do_part, far=do_far, own=do_own, side=do_side, middle=do_middle, zfar=do_zfar,
        zown=do_zown, zmid=do_zmid, cores=do_cores, place=do_place, finish=do_finish_sum,
        attend=do_attend,
    )
    for name, *which in REDUCE:
        with jax.named_scope("_".join([name] + [str(w) for w in which])):
            steps[name](*which)
    checked = recv_a[sec[s * MB] >> 3].astype(F32)
    for p in range(NP):
        late[p].wait_recv()
    mine = fb[0]
    theirs = finr[...]
    meansq = jnp.sum(mine * mine, axis=-1, keepdims=True)
    meansq = (meansq + jnp.sum(theirs * theirs, axis=-1, keepdims=True)) / D
    scale = lax.rsqrt(meansq + EPS)
    outb[c] = mine
    outb[o] = theirs
    for h in range(2):
        cols_of = slice(h * H, (h + 1) * H)
        checkb[:, cols_of] = (checked[:, cols_of] + outb[h] * scale * gpost[:, cols_of]).astype(BF16)
    for copy in pending:
        copy.wait_send()


def put_out(moved, newacc, check, moved_hbm, newacc_hbm, check_hbm, sem):
    copies = [
        pltpu.make_async_copy(source, into, sem.at[i])
        for i, (source, into) in enumerate(
            ((newacc, newacc_hbm), (moved, moved_hbm), (check, check_hbm))
        )
    ]
    for copy in copies:
        copy.start()
    for copy in copies:
        copy.wait()


def on_device(act, sec, acc, blk, loss, gpre, wq, wkv, wo, gpost):
    tab = jnp.asarray(rotary_tables())
    any_ = pl.BlockSpec(memory_space=pl.ANY)
    vmem = pl.BlockSpec(memory_space=pltpu.VMEM)
    V = pltpu.VMEM
    dma = pltpu.SemaphoreType.DMA
    moved, newacc, check = pl.pallas_call(
        kernel,
        out_shape=(
            V((MB, ROWS, D), BF16),
            V((BLK, 2, D), F32),
            V((ROWS, D), BF16),
        ),
        in_specs=[pl.BlockSpec(memory_space=pltpu.HBM)] * 11,
        out_specs=(vmem, vmem, vmem),
        scratch_shapes=[
            V((MB, ROWS, D), BF16), V((NS, ROWS, D), BF16), V((NS, ROWS, D), BF16),
            V((BLK, 2, D), F32),
            V((NY, NZ, 2, 2, D), BF16), V((NY, NZ, 2, 2, D), BF16),
            V((NZ, NY, 2, 2, D), BF16), V((NZ, NY, 2, D), BF16), V((2, 2, 2, 2, D), BF16),
            V((1, HD), F32), V((4, 1, HD), F32), V((1, HD), F32), V((4, 1, HD), F32),
            V((1, HD), F32), V((1, HD), F32),
            V((2, ROWS, H), BF16), V((NY, NZ, 2, ROWS, H), BF16), V((H, 4 * HD), BF16),
            V((2, HD, H), BF16), V((4, 4, 128, HD), F32), V((4, 128, HD), F32),
            V((4, 2, 128, HD), F32), V((NY, NZ, 32, HD), BF16), V((NY, NZ, 32, HD), BF16),
            V((NY, NZ, 32, HD), BF16), V((2, 4, 128, HD), BF16),
            V((NY, NZ, 2, ROWS, H), BF16), V((4, 2, ROWS, H), BF16), V((4, 2, ROWS, H), BF16),
            V((4, 2, ROWS, H), BF16), V((2, ROWS, H), BF16), V((2, ROWS, H), BF16),
            V((2, ROWS, H), BF16), V((3, 2, ROWS, H), BF16), V((2, ROWS, H), F32),
            V((ROWS, H), F32), V((2, ROWS, H), F32),
            V((2, NY, NZ, 32, HD), F32), pltpu.SMEM((64,), jnp.int32),
            pltpu.SMEM((1024,), jnp.int32), V((1, 1), F32), V((1, D), F32), V((1, D), F32),
            V((2, 2, ROWS, H), BF16),
            dma((15,)), dma((NP,)), dma((NP,)), dma((2, 2, NP)), dma((2, 2, NP)), dma((NS,)), dma((NS,)), dma((16,)), dma((16,)), dma((2, 3, NP)), dma((2, 3, NP)),
            dma((4, 2, 3, NP)), dma((4, 2, 3, NP)), dma((17,)), dma((17,)),
            dma((4, 2, 3, NP)), dma((4, 2, 3, NP)), dma((3, 2, NP)), dma((3, 2, NP)), dma((4,)), dma((4,)),
        ],
        compiler_params=pltpu.CompilerParams(
            collective_id=0, has_side_effects=True, vmem_limit_bytes=61 * 1024 * 1024
        ),
        name="restore",
    )(sec, blk, act, acc, loss, gpre, wq[0], wkv[0], wo[0], gpost, tab)
    moved, newacc, check = pl.pallas_call(
        put_out,
        out_shape=(
            jax.ShapeDtypeStruct((MB, ROWS, D), BF16),
            jax.ShapeDtypeStruct((BLK, 2, D), F32),
            jax.ShapeDtypeStruct((ROWS, D), BF16),
        ),
        in_specs=[vmem] * 3,
        out_specs=(any_, any_, any_),
        scratch_shapes=[dma((3,))],
        compiler_params=pltpu.CompilerParams(vmem_limit_bytes=8 * 1024 * 1024),
        name="put_out",
    )(moved, newacc, check)
    return moved, newacc, check[None]


def solution(mesh):
    placed = (
        P("section", "dp", None),
        P(),
        P("dp", "section", None),
        P(),
        P("section", "dp"),
        P("section", None),
        P("section", None, "dp"),
        P("section", None, "dp"),
        P("section", "dp", None),
        P("section", None),
    )
    return jax.shard_map(
        on_device,
        mesh=mesh,
        in_specs=placed,
        out_specs=(P("section", "dp", None), P("dp", "section", None), P("section", "dp", None)),
        check_vma=False,
    )
```

time: 89.7 us -> 83.4 us (0.930)
  the two profiles are of different devices: /device:TPU:1 before, /device:TPU:35 now
where the time goes in v3:
time: 83.4 us; the launch traced here: 83.3 us
  Pallas kernels  82 us (98%)
  between operations  1.29 us (2%)
    pallas_call x1, Pallas kernels, on_device(): pl.pallas_call(kernel, out_shape=(V((MB, ROWS, D), BF16), V((BLK, 2, D),...  80.6 us

profile of v3, /device:TPU:35, one launch (start us, length us, event | category | flops | bytes accessed | tf_op | source)
XLA Modules:
  0.0 83.3 jit_solution(14894946761371932837)
XLA Ops:
  1.3 80.6 %restore.1 = (bf16[8,16,4608]{2,1,0:T(8,128)(2,1)S(1)}, f32[32,2,4608]{2,1,0:T(2,128)S(1)}, bf16[16,4608]{1,0:T(8,128)(2,1)S(1)}) custom-call(s32[64]{0:T(128)} %sec_hbm.1, s32[1024]{0:T(1024)} %blk_hbm.1, bf16[8,16,4608]{2,1,0:T(8,128)(2,1)} %act_hbm.1, f32[32,2,4608]{2,1,0:T(2,128)} %acc_hbm.1, f32[1,1]{1,0:T(1,128)S(6)} %copy.14.loss_hbm, ...), custom_call_target="tpu_custom_call" | custom-call | tf_op jit(solution)/shard_map/restore/pallas_call | solution.py:512
  81.9 1.5 %put_out.1 = (bf16[8,16,4608]{2,1,0:T(8,128)(2,1)}, f32[32,2,4608]{2,1,0:T(2,128)}, bf16[16,4608]{1,0:T(8,128)(2,1)}) custom-call(bf16[8,16,4608]{2,1,0:T(8,128)(2,1)S(1)} %get-tuple-element.9.moved, f32[32,2,4608]{2,1,0:T(2,128)S(1)} %get-tuple-element.10.newacc, bf16[16,4608]{1,0:T(8,128)(2,1)S(1)} %get-tuple-element.11.check), custom_call_target="tpu_custom_call" | custom-call | tf_op jit(solution)/shard_map/put_out/pallas_call | solution.py:548

commit v4 on v3

--- a/solution.py
+++ b/solution.py
@@ -21,20 +21,22 @@
 EPS = 1e-06
 NP = 2
 HP = H // NP
+HW = H + 128
 F32 = jnp.float32
 BF16 = jnp.bfloat16
 
 GATHER = (
-    ("near", 0, 1), ("row", 0, 0, 1), ("row", 0, 0, 0), ("near", 0, 0), ("near", 1, 1),
-    ("row", 0, 1, 0), ("row", 0, 1, 1), ("near", 1, 0), ("ony", 0, 0, 1), ("ony", 0, 0, 0),
-    ("row", 1, 0, 1), ("ony", 0, 1, 0), ("ony", 0, 1, 1), ("row", 2, 0, 1), ("row", 1, 0, 0),
-    ("row", 2, 0, 0), ("onz", 0, 0), ("onz", 0, 1), ("row", 2, 1, 1), ("row", 1, 1, 1),
-    ("moved",), ("onz", 1, 1), ("onz", 1, 0), ("ony", 2, 0, 1), ("project", 0), ("row", 1, 1, 0),
-    ("ony", 1, 0, 1), ("row", 2, 1, 0), ("blocks",), ("row", 3, 1, 1), ("ony", 1, 0, 0),
-    ("ony", 1, 1, 1), ("ony", 1, 1, 0), ("ony", 2, 1, 1), ("row", 3, 1, 0), ("ony", 2, 1, 0),
-    ("row", 3, 0, 0), ("row", 3, 0, 1), ("ony", 2, 0, 0), ("ony", 3, 1, 1), ("ony", 3, 1, 0),
-    ("relay",), ("ony", 3, 0, 0), ("ony", 3, 0, 1), ("project", 1), ("finish", 0), ("project", 2),
-    ("project", 3), ("finish", 1), ("finish", 2), ("finish", 3),
+    ("near", 0, 0), ("row", 0, 0, 0), ("row", 0, 1, 0), ("near", 1, 0), ("ony", 0, 0, 0),
+    ("ony", 0, 1, 0), ("row", 2, 0, 0), ("row", 1, 0, 0), ("scaled", 1), ("near", 0, 1),
+    ("row", 0, 0, 1), ("row", 0, 1, 1), ("near", 1, 1), ("row", 1, 1, 0), ("row", 2, 1, 0),
+    ("onz", 1, 0), ("ony", 0, 0, 1), ("ony", 1, 0, 0), ("onz", 0, 1), ("ony", 0, 1, 1),
+    ("onz", 0, 0), ("ony", 2, 0, 0), ("row", 1, 0, 1), ("row", 1, 1, 1), ("onz", 1, 1),
+    ("row", 2, 1, 1), ("row", 2, 0, 1), ("blocks",), ("project", 0), ("ony", 1, 0, 1),
+    ("row", 3, 1, 0), ("finish", 0), ("moved",), ("ony", 1, 1, 0), ("row", 3, 1, 1),
+    ("ony", 1, 1, 1), ("ony", 2, 1, 0), ("ony", 2, 1, 1), ("row", 3, 0, 1), ("row", 3, 0, 0),
+    ("ony", 2, 0, 1), ("relay",), ("ony", 3, 1, 0), ("ony", 3, 1, 1), ("ony", 3, 0, 0),
+    ("ony", 3, 0, 1), ("project", 1), ("project", 2), ("project", 3), ("finish", 1),
+    ("finish", 2), ("finish", 3),
 )
 
 REDUCE = (
@@ -69,12 +71,13 @@
 def kernel(
     sec_hbm, blk_hbm, act_hbm, acc_hbm, loss_hbm, gpre_hbm, wq_hbm, wkv_hbm, wo_hbm, gpost_hbm, tab_hbm,
     moved_v, newacc_v, checkb,
-    act_v, asend, recv_a, acc_v, bsend, b1, b2, b3, bre,
+    act_v, asend, recv_a0, recv_a1, acc_v, bsend, b1, b2, b3, bre,
     lsend, lry, lsum, lrz, lfin, lrc,
     nbuf, xh, wbuf, wobuf, rbuf, rrq, rrkv, qf, kf, vf, at2,
     pbuf, yrh, yro, yrm, zrh, zro, zrm, zs, fb, finr, outb, tab, sec, blk, loss_ref, gpre, gpost,
     zrs, loc, df_s, df_r, dx_s, dx_r, a_s, a_r, bl_s, bl_r, cz_s, cz_r, cy_s, cy_r, cc_s, cc_r, dy_s, dy_r, dz_s, dz_r, bz_s, bz_r,
 ):
+    recv_a = (recv_a0, recv_a1)
     s = lax.axis_index("section")
     d = lax.axis_index("dp")
     y = lax.div(d, 8)
@@ -155,17 +158,24 @@
         for j in range(MB):
             source = sec[to * MB + j]
             at = at + jnp.where((source >> 3) == s, source & 7, 0)
-        if r == 0:
-            recv_a[s] = act_v[at]
-        else:
-            asend[r] = act_v[at]
+        chosen = act_v[at]
+        for p in range(NP):
+            for h in range(2):
+                first = h * H + p * HP
+                if r == 0:
+                    recv_a[p][s, h] = chosen[:, first : first + HP]
+                else:
+                    asend[r, p, h] = chosen[:, first : first + HP]
     lsend[...] = jnp.broadcast_to(loss_ref[...], (1, HD))
 
     pl.semaphore_wait(barrier, len(greet))
 
-    from_s = [
-        remote(asend.at[r], recv_a.at[s], a_s.at[r], a_r.at[r], at_s[r]) for r in range(1, NS)
-    ]
+    from_s = {}
+    for p in range(NP):
+        for r in range(1, NS):
+            from_s[p, r] = remote(
+                asend.at[r, p], recv_a[p].at[s], a_s.at[r, p], a_r.at[r, p], at_s[r]
+            )
     from_ly = [
         remote(lsend, lry.at[r], bl_s.at[8 + r], bl_r.at[8 + r], at_y[r]) for r in (1, 2, 3)
     ]
@@ -196,21 +206,38 @@
                 remote(bsend.at[r], b1.at[r], bl_s.at[r], bl_r.at[r], at_y[r])
             )
 
-    for copy in from_s:
-        copy.wait_recv()
-    x = recv_a[sec[s * MB] >> 3]
-    xf = x.astype(F32)
-    meansq = jnp.mean(xf * xf, axis=-1, keepdims=True)
-    normed = (xf * lax.rsqrt(meansq + EPS) * gpre[...]).astype(BF16)
-    nbuf[0] = normed[:, :H]
-    nbuf[1] = normed[:, H:]
-    xh[y, z, c] = nbuf[c]
-    core_n = remote(nbuf.at[o], xh.at[y, z, c], cc_s.at[3], cc_r.at[3], at_c)
-
+    def lanes(p):
+        return pl.ds(p * HP, HP if p < NP - 1 else HW - p * HP)
+
+    squares, core_n = [], {}
+
+    def do_scaled(p):
+        for r in range(1, NS):
+            from_s[p, r].wait_recv()
+        x = recv_a[p][sec[s * MB] >> 3]
+        for h in range(2):
+            xf = x[h].astype(F32)
+            squares.append(jnp.sum(xf * xf, axis=-1, keepdims=True))
+            first = h * H + p * HP
+            nbuf[h, :, p * HP : (p + 1) * HP] = (xf * gpre[:, first : first + HP]).astype(BF16)
+        if p == NP - 1:
+            scale = lax.rsqrt(sum(squares) / D + EPS)
+            high_part = scale.astype(BF16).astype(F32)
+            lane = lax.broadcasted_iota(jnp.int32, (ROWS, 128), 1)
+            both = jnp.where(lane < 64, high_part, scale - high_part).astype(BF16)
+            nbuf[0, :, H:] = both
+            nbuf[1, :, H:] = both
+        xh[y, z, c, :, lanes(p)] = nbuf[c, :, lanes(p)]
+        core_n[p] = remote(
+            nbuf.at[o, :, lanes(p)], xh.at[y, z, c, :, lanes(p)],
+            df_s.at[NP + p], df_r.at[NP + p], at_c,
+        )
+
+    do_scaled(0)
     half = (c, o)
 
     def piece_of(yy, zz, i, p):
-        return xh.at[yy, zz, half[i], :, pl.ds(p * HP, HP)]
+        return xh.at[yy, zz, half[i], :, lanes(p)]
 
     order = [z, zb, za, zf]
     near_z, far_z, rows_y, rows_on = {}, {}, {}, {}
@@ -259,7 +286,7 @@
             for p in range(NP):
                 rows_y[q, i, p, 1 - i].wait_recv()
                 rows_on[q, i, p].wait_recv()
-        rows = xh[:, zz].reshape(128, H)
+        rows = xh[:, zz, :, :, 0:H].reshape(128, H)
         res = jnp.dot(rows, wbuf[...], preferred_element_type=F32)
         for j in range(4):
             rbuf[q, j] = res[:, j * HD : (j + 1) * HD]
@@ -274,9 +301,11 @@
             copy.wait_recv()
         cosine = tab[0, :, zz].reshape(128, HD)
         sine = tab[1, :, zz].reshape(128, HD)
-        query = rbuf[q, c] + rrq[zz]
-        key = rbuf[q, 2] + rrkv[zz, 0]
-        value = rbuf[q, 3] + rrkv[zz, 1]
+        parts = xh[:, zz, :, :, H:HW].reshape(128, 128).astype(F32)
+        scale = parts[:, 0:1] + parts[:, 64:65]
+        query = (rbuf[q, c] + rrq[zz]) * scale
+        key = (rbuf[q, 2] + rrkv[zz, 0]) * scale
+        value = (rbuf[q, 3] + rrkv[zz, 1]) * scale
         query = query * cosine + pltpu.roll(query, HD // 2, 1) * sine
         key = key * cosine + pltpu.roll(key, HD // 2, 1) * sine
         qf[:, zz] = query.astype(BF16).reshape(NY, 32, HD)
@@ -314,18 +343,20 @@
 
     def do_moved():
         for j in range(MB):
-            moved_v[j] = recv_a[sec[s * MB + j] >> 3]
+            for p in range(NP):
+                rows = recv_a[p][sec[s * MB + j] >> 3]
+                for h in range(2):
+                    moved_v[j, :, h * H + p * HP : h * H + (p + 1) * HP] = rows[h]
 
     steps = dict(
         near=do_near, row=do_row, onz=do_onz, ony=do_ony, project=do_project,
         finish=do_finish, blocks=do_blocks, relay=do_relay, moved=do_moved,
+        scaled=do_scaled,
     )
-    waited = False
     for name, *which in GATHER:
-        second = (name == "near" and which[0] == 1) or (name == "row" and which[:2] == [0, 1])
-        if second and not waited:
-            core_n.wait_recv()
-            waited = True
+        if (name == "near" or (name == "row" and which[0] == 0)) and which[-2] == 1:
+            if which[-1] in core_n:
+                core_n.pop(which[-1]).wait_recv()
         with jax.named_scope("_".join([name] + [str(w) for w in which])):
             steps[name](*which)
     back = [zf, zb, za, z]
@@ -473,7 +504,7 @@
     for name, *which in REDUCE:
         with jax.named_scope("_".join([name] + [str(w) for w in which])):
             steps[name](*which)
-    checked = recv_a[sec[s * MB] >> 3].astype(F32)
+    checked = [recv_a[p][sec[s * MB] >> 3].astype(F32) for p in range(NP)]
     for p in range(NP):
         late[p].wait_recv()
     mine = fb[0]
@@ -484,8 +515,10 @@
     outb[c] = mine
     outb[o] = theirs
     for h in range(2):
-        cols_of = slice(h * H, (h + 1) * H)
-        checkb[:, cols_of] = (checked[:, cols_of] + outb[h] * scale * gpost[:, cols_of]).astype(BF16)
+        for p in range(NP):
+            cols_of = slice(h * H + p * HP, h * H + (p + 1) * HP)
+            change = outb[h, :, p * HP : (p + 1) * HP] * scale * gpost[:, cols_of]
+            checkb[:, cols_of] = (checked[p][h] + change).astype(BF16)
     for copy in pending:
         copy.wait_send()
 
@@ -519,13 +552,14 @@
         in_specs=[pl.BlockSpec(memory_space=pltpu.HBM)] * 11,
         out_specs=(vmem, vmem, vmem),
         scratch_shapes=[
-            V((MB, ROWS, D), BF16), V((NS, ROWS, D), BF16), V((NS, ROWS, D), BF16),
+            V((MB, ROWS, D), BF16), V((NS, NP, 2, ROWS, HP), BF16),
+            V((NS, 2, ROWS, HP), BF16), V((NS, 2, ROWS, HP), BF16),
             V((BLK, 2, D), F32),
             V((NY, NZ, 2, 2, D), BF16), V((NY, NZ, 2, 2, D), BF16),
             V((NZ, NY, 2, 2, D), BF16), V((NZ, NY, 2, D), BF16), V((2, 2, 2, 2, D), BF16),
             V((1, HD), F32), V((4, 1, HD), F32), V((1, HD), F32), V((4, 1, HD), F32),
             V((1, HD), F32), V((1, HD), F32),
-            V((2, ROWS, H), BF16), V((NY, NZ, 2, ROWS, H), BF16), V((H, 4 * HD), BF16),
+            V((2, ROWS, HW), BF16), V((NY, NZ, 2, ROWS, HW), BF16), V((H, 4 * HD), BF16),
             V((2, HD, H), BF16), V((4, 4, 128, HD), F32), V((4, 128, HD), F32),
             V((4, 2, 128, HD), F32), V((NY, NZ, 32, HD), BF16), V((NY, NZ, 32, HD), BF16),
             V((NY, NZ, 32, HD), BF16), V((2, 4, 128, HD), BF16),
@@ -536,7 +570,7 @@
             V((2, NY, NZ, 32, HD), F32), pltpu.SMEM((64,), jnp.int32),
             pltpu.SMEM((1024,), jnp.int32), V((1, 1), F32), V((1, D), F32), V((1, D), F32),
             V((2, 2, ROWS, H), BF16),
-            dma((15,)), dma((NP,)), dma((NP,)), dma((2, 2, NP)), dma((2, 2, NP)), dma((NS,)), dma((NS,)), dma((16,)), dma((16,)), dma((2, 3, NP)), dma((2, 3, NP)),
+            dma((15,)), dma((2 * NP,)), dma((2 * NP,)), dma((2, 2, NP)), dma((2, 2, NP)), dma((NS, NP)), dma((NS, NP)), dma((16,)), dma((16,)), dma((2, 3, NP)), dma((2, 3, NP)),
             dma((4, 2, 3, NP)), dma((4, 2, 3, NP)), dma((17,)), dma((17,)),
             dma((4, 2, 3, NP)), dma((4, 2, 3, NP)), dma((3, 2, NP)), dma((3, 2, NP)), dma((4,)), dma((4,)),
         ],

time: 83.4 us -> 82.3 us (0.987)
  the two profiles are of different devices: /device:TPU:35 before, /device:TPU:1 now
where the time goes in v4:
time: 82.3 us; the launch traced here: 82.2 us
  Pallas kernels  80.9 us (98%)
  between operations  1.29 us (2%)
    pallas_call x1, Pallas kernels, on_device(): pl.pallas_call(kernel, out_shape=(V((MB, ROWS, D), BF16), V((BLK, 2, D),...  79.4 us

profile of v4, /device:TPU:1, one launch (start us, length us, event | category | flops | bytes accessed | tf_op | source)
XLA Modules:
  0.0 82.2 jit_solution(17623697272389370557)
XLA Ops:
  1.3 79.4 %restore.1 = (bf16[8,16,4608]{2,1,0:T(8,128)(2,1)S(1)}, f32[32,2,4608]{2,1,0:T(2,128)S(1)}, bf16[16,4608]{1,0:T(8,128)(2,1)S(1)}) custom-call(s32[64]{0:T(128)} %sec_hbm.1, s32[1024]{0:T(1024)} %blk_hbm.1, bf16[8,16,4608]{2,1,0:T(8,128)(2,1)} %act_hbm.1, f32[32,2,4608]{2,1,0:T(2,128)} %acc_hbm.1, f32[1,1]{1,0:T(1,128)S(6)} %copy.14.loss_hbm, ...), custom_call_target="tpu_custom_call" | custom-call | tf_op jit(solution)/shard_map/restore/pallas_call | solution.py:545
  80.7 1.5 %put_out.1 = (bf16[8,16,4608]{2,1,0:T(8,128)(2,1)}, f32[32,2,4608]{2,1,0:T(2,128)}, bf16[16,4608]{1,0:T(8,128)(2,1)}) custom-call(bf16[8,16,4608]{2,1,0:T(8,128)(2,1)S(1)} %get-tuple-element.9.moved, f32[32,2,4608]{2,1,0:T(2,128)S(1)} %get-tuple-element.10.newacc, bf16[16,4608]{1,0:T(8,128)(2,1)S(1)} %get-tuple-element.11.check), custom_call_target="tpu_custom_call" | custom-call | tf_op jit(solution)/shard_map/put_out/pallas_call | solution.py:582

commit v5 on v4

--- a/solution.py
+++ b/solution.py
@@ -31,30 +31,30 @@
     ("row", 0, 0, 1), ("row", 0, 1, 1), ("near", 1, 1), ("row", 1, 1, 0), ("row", 2, 1, 0),
     ("onz", 1, 0), ("ony", 0, 0, 1), ("ony", 1, 0, 0), ("onz", 0, 1), ("ony", 0, 1, 1),
     ("onz", 0, 0), ("ony", 2, 0, 0), ("row", 1, 0, 1), ("row", 1, 1, 1), ("onz", 1, 1),
-    ("row", 2, 1, 1), ("row", 2, 0, 1), ("blocks",), ("project", 0), ("ony", 1, 0, 1),
-    ("row", 3, 1, 0), ("finish", 0), ("moved",), ("ony", 1, 1, 0), ("row", 3, 1, 1),
-    ("ony", 1, 1, 1), ("ony", 2, 1, 0), ("ony", 2, 1, 1), ("row", 3, 0, 1), ("row", 3, 0, 0),
-    ("ony", 2, 0, 1), ("relay",), ("ony", 3, 1, 0), ("ony", 3, 1, 1), ("ony", 3, 0, 0),
-    ("ony", 3, 0, 1), ("project", 1), ("project", 2), ("project", 3), ("finish", 1),
-    ("finish", 2), ("finish", 3),
+    ("row", 2, 1, 1), ("row", 2, 0, 1), ("blocks",), ("ony", 1, 0, 1), ("row", 3, 1, 0),
+    ("moved",), ("ony", 1, 1, 0), ("row", 3, 1, 1), ("ony", 1, 1, 1), ("ony", 2, 1, 0),
+    ("ony", 2, 1, 1), ("row", 3, 0, 1), ("row", 3, 0, 0), ("ony", 2, 0, 1), ("ony", 3, 1, 0),
+    ("ony", 3, 1, 1), ("project", 0), ("ony", 3, 0, 0), ("ony", 3, 0, 1), ("project", 1),
+    ("project", 2), ("finish", 0), ("project", 3), ("finish", 1), ("finish", 2), ("finish", 3),
+    ("relay",),
 )
 
 REDUCE = (
-    ("part", 0), ("far", 0, 0, 0), ("far", 0, 0, 1), ("part", 1), ("far", 1, 0, 0),
-    ("side", 1, 1, 0), ("side", 1, 0, 0), ("attend", 3), ("own", 0, 0, 0), ("side", 1, 0, 1),
-    ("side", 1, 1, 1), ("far", 0, 1, 0), ("far", 1, 1, 0), ("far", 0, 1, 1), ("middle", 0, 0, 0),
-    ("far", 1, 0, 1), ("part", 2), ("own", 0, 1, 1), ("far", 2, 0, 0), ("own", 0, 1, 0),
-    ("side", 2, 1, 0), ("side", 2, 1, 1), ("middle", 0, 1, 0), ("own", 0, 0, 1), ("part", 3),
-    ("middle", 0, 0, 1), ("side", 2, 0, 1), ("zfar", 0, 0), ("cores",), ("middle", 0, 1, 1),
-    ("side", 2, 0, 0), ("far", 2, 1, 1), ("middle", 2, 0, 0), ("middle", 1, 0, 0), ("zfar", 1, 0),
-    ("far", 1, 1, 1), ("middle", 1, 0, 1), ("zfar", 0, 1), ("far", 2, 1, 0), ("middle", 1, 1, 0),
-    ("zfar", 1, 1), ("middle", 2, 1, 1), ("far", 2, 0, 1), ("far", 3, 1, 1), ("far", 3, 0, 0),
-    ("zmid", 0, 0), ("zown", 0, 0), ("middle", 1, 1, 1), ("middle", 2, 1, 0), ("far", 3, 1, 0),
-    ("own", 3, 0, 0), ("zown", 0, 1), ("zmid", 1, 0), ("middle", 2, 0, 1), ("far", 3, 0, 1),
-    ("zown", 1, 1), ("middle", 3, 0, 0), ("own", 3, 1, 1), ("own", 3, 1, 0), ("zmid", 1, 1),
-    ("place",), ("middle", 3, 1, 0), ("middle", 3, 1, 1), ("zown", 1, 0), ("own", 3, 0, 1),
-    ("zmid", 0, 1), ("middle", 3, 0, 1), ("finish", 1, 1), ("finish", 0, 0), ("finish", 1, 0),
-    ("finish", 0, 1),
+    ("attend", 1), ("part", 0), ("far", 0, 0, 0), ("far", 0, 0, 1), ("own", 0, 1, 0),
+    ("own", 0, 1, 1), ("far", 0, 1, 0), ("far", 0, 1, 1), ("own", 0, 0, 0), ("own", 0, 0, 1),
+    ("attend", 2), ("part", 1), ("far", 1, 0, 0), ("side", 1, 1, 0), ("side", 1, 0, 0),
+    ("attend", 3), ("side", 1, 0, 1), ("side", 1, 1, 1), ("far", 1, 1, 0), ("middle", 0, 0, 0),
+    ("far", 1, 0, 1), ("part", 2), ("far", 2, 0, 0), ("side", 2, 1, 0), ("side", 2, 1, 1),
+    ("middle", 0, 1, 0), ("part", 3), ("middle", 0, 0, 1), ("side", 2, 0, 1), ("zfar", 0, 0),
+    ("middle", 0, 1, 1), ("side", 2, 0, 0), ("far", 2, 1, 1), ("middle", 2, 0, 0),
+    ("middle", 1, 0, 0), ("zfar", 1, 0), ("far", 1, 1, 1), ("middle", 1, 0, 1), ("zfar", 0, 1),
+    ("far", 2, 1, 0), ("middle", 1, 1, 0), ("zfar", 1, 1), ("middle", 2, 1, 1), ("far", 2, 0, 1),
+    ("far", 3, 1, 1), ("far", 3, 0, 0), ("zown", 0, 0), ("middle", 1, 1, 1), ("middle", 2, 1, 0),
+    ("far", 3, 1, 0), ("own", 3, 0, 0), ("zown", 0, 1), ("zmid", 1, 0), ("cores",),
+    ("zmid", 0, 0), ("middle", 2, 0, 1), ("far", 3, 0, 1), ("zown", 1, 1), ("middle", 3, 0, 0),
+    ("own", 3, 1, 1), ("own", 3, 1, 0), ("zmid", 1, 1), ("middle", 3, 1, 0), ("middle", 3, 1, 1),
+    ("zown", 1, 0), ("own", 3, 0, 1), ("zmid", 0, 1), ("middle", 3, 0, 1), ("place",),
+    ("finish", 1, 1), ("finish", 0, 0), ("finish", 1, 0), ("finish", 0, 1),
 )
 
 
@@ -381,8 +381,7 @@
             at2.at[c, zz], at2.at[c, zz], cc_s.at[12 + zz], cc_r.at[12 + zz], at_c
         )
 
-    for m in range(3):
-        do_attend(m)
+    do_attend(0)
 
     y_far, y_own, y_mid, z_side, z_far, z_own, z_mid, late = {}, {}, {}, {}, {}, {}, {}, {}
 

time: 82.3 us -> 80.5 us (0.978)
  Pallas kernels: 80.9 us -> 79.1 us
    pallas_call x1, Pallas kernels: 79.4 us -> 77.6 us  [on_device(): pl.pallas_call(kernel, out_shape=(V((MB, ROWS, D), BF16), V((BLK, 2, D),...]
where the time goes in v5:
time: 80.5 us; the launch traced here: 80.4 us
  Pallas kernels  79.1 us (98%)
  between operations  1.29 us (2%)
    pallas_call x1, Pallas kernels, on_device(): pl.pallas_call(kernel, out_shape=(V((MB, ROWS, D), BF16), V((BLK, 2, D),...  77.6 us

profile of v5, /device:TPU:1, one launch (start us, length us, event | category | flops | bytes accessed | tf_op | source)
XLA Modules:
  0.0 80.4 jit_solution(14458179239343624493)
XLA Ops:
  1.3 77.6 %restore.1 = (bf16[8,16,4608]{2,1,0:T(8,128)(2,1)S(1)}, f32[32,2,4608]{2,1,0:T(2,128)S(1)}, bf16[16,4608]{1,0:T(8,128)(2,1)S(1)}) custom-call(s32[64]{0:T(128)} %sec_hbm.1, s32[1024]{0:T(1024)} %blk_hbm.1, bf16[8,16,4608]{2,1,0:T(8,128)(2,1)} %act_hbm.1, f32[32,2,4608]{2,1,0:T(2,128)} %acc_hbm.1, f32[1,1]{1,0:T(1,128)S(6)} %copy.14.loss_hbm, ...), custom_call_target="tpu_custom_call" | custom-call | tf_op jit(solution)/shard_map/restore/pallas_call | solution.py:544
  78.9 1.5 %put_out.1 = (bf16[8,16,4608]{2,1,0:T(8,128)(2,1)}, f32[32,2,4608]{2,1,0:T(2,128)}, bf16[16,4608]{1,0:T(8,128)(2,1)}) custom-call(bf16[8,16,4608]{2,1,0:T(8,128)(2,1)S(1)} %get-tuple-element.9.moved, f32[32,2,4608]{2,1,0:T(2,128)S(1)} %get-tuple-element.10.newacc, bf16[16,4608]{1,0:T(8,128)(2,1)S(1)} %get-tuple-element.11.check), custom_call_target="tpu_custom_call" | custom-call | tf_op jit(solution)/shard_map/put_out/pallas_call | solution.py:581
